TPU v7x, 16 devices: a whole 2x2x2 slice. The times are simulated.
16 devices in a mesh: ep: 16 (over z, y, x, core).
Axes of the slice: x: 2, y: 2, z: 2, core: 2. Of those that a mesh axis runs over, the one named last changes fastest.
Arguments:
- tokens: bfloat16 [16384, 768], P('ep')
- grad_out: bfloat16 [16384, 768], P('ep')
- expert_ids: int32 [16384, 2], P('ep')
- w_gate: bfloat16 [768, 16], replicated
- w_in: bfloat16 [16, 768, 3072], P('ep')
- w_out: bfloat16 [16, 3072, 768], P('ep')
Outputs:
- output 1: bfloat16 [16384, 768], P('ep')
- output 2: bfloat16 [16384, 768], P('ep')
- output 3: float32 [16, 768, 3072], P('ep')
- output 4: float32 [16, 3072, 768], P('ep')
- output 5: float32 [768, 16], replicated
All inputs are finite; a program needn't handle non-finite values.
Results may differ from a plain program's by a relative error of at most 0.00483528.
Values are sent between devices in bfloat16 or wider.
A program may use at most 1 GiB of HBM per device.

v0:
```python
import jax
import jax.numpy as jnp
from jax import lax
from jax.sharding import PartitionSpec as P


def route_slots(expert_ids, n_exp):
    flat_ids = expert_ids.reshape(-1)
    one_hot = (flat_ids[:, None] == jnp.arange(n_exp)[None, :]).astype(jnp.int32)
    rank_in = jnp.sum((jnp.cumsum(one_hot, axis=0) - one_hot) * one_hot, axis=1)
    return flat_ids, one_hot, rank_in


def slot_owner(dest_slot, n_slots):
    n_choice = dest_slot.shape[0]
    return jnp.full((n_slots,), n_choice, jnp.int32).at[dest_slot].set(jnp.arange(n_choice, dtype=jnp.int32), mode='drop')


def local_block(tokens, grad_out, expert_ids, w_gate, w_in, w_out):
    n_exp = w_gate.shape[1]
    tok_dev, d_model = tokens.shape
    cap_rows = tok_dev // 4
    n_choice = 2 * tok_dev
    n_slots = n_exp * cap_rows
    w_one = w_in[0]
    w_two = w_out[0]
    flat_ids, one_hot, rank_in = route_slots(expert_ids, n_exp)
    dest_slot = flat_ids * cap_rows + rank_in
    src_choice = slot_owner(dest_slot, n_slots)
    zero_row = jnp.zeros((1, d_model), jnp.bfloat16)
    x_table = jnp.concatenate([tokens, zero_row], axis=0)
    send_x = jnp.take(x_table, jnp.where(src_choice < n_choice, src_choice // 2, tok_dev), axis=0)
    recv_x = lax.all_to_all(send_x.reshape(n_exp, cap_rows, d_model), 'ep', 0, 0, tiled=True).reshape(n_slots, d_model)
    a_pre = jnp.dot(recv_x, w_one, preferred_element_type=jnp.float32)
    hidden, gelu_vjp = jax.vjp(jax.nn.gelu, a_pre)
    hid_b = hidden.astype(jnp.bfloat16)
    y_rows = jnp.dot(hid_b, w_two, preferred_element_type=jnp.float32).astype(jnp.bfloat16)
    y_back = lax.all_to_all(y_rows.reshape(n_exp, cap_rows, d_model), 'ep', 0, 0, tiled=True).reshape(n_slots, d_model)
    y_pair = jnp.take(y_back, dest_slot, axis=0).reshape(tok_dev, 2, d_model)
    logits = jnp.dot(tokens, w_gate, preferred_element_type=jnp.float32)
    choice_hot = one_hot.reshape(tok_dev, 2, n_exp) > 0
    sel_logit = jnp.sum(jnp.where(choice_hot, logits[:, None, :], 0.0), axis=-1)
    gate_val = jax.nn.softmax(sel_logit, axis=1)
    y_out = jnp.sum(gate_val[:, :, None] * y_pair.astype(jnp.float32), axis=1).astype(jnp.bfloat16)
    d_gate = jnp.einsum('tm,tkm->tk', grad_out, y_pair, preferred_element_type=jnp.float32)
    dy_flat = (gate_val[:, :, None] * grad_out[:, None, :].astype(jnp.float32)).astype(jnp.bfloat16).reshape(n_choice, d_model)
    send_dy = jnp.take(jnp.concatenate([dy_flat, zero_row], axis=0), src_choice, axis=0)
    recv_dy = lax.all_to_all(send_dy.reshape(n_exp, cap_rows, d_model), 'ep', 0, 0, tiled=True).reshape(n_slots, d_model)
    g_w_out = jnp.einsum('rh,rm->hm', hid_b, recv_dy, preferred_element_type=jnp.float32)
    d_hid = jnp.einsum('rm,hm->rh', recv_dy, w_two, preferred_element_type=jnp.float32)
    d_pre = gelu_vjp(d_hid)[0].astype(jnp.bfloat16)
    g_w_in = jnp.einsum('rm,rh->mh', recv_x, d_pre, preferred_element_type=jnp.float32)
    dx_rows = jnp.einsum('rh,mh->rm', d_pre, w_one, preferred_element_type=jnp.float32).astype(jnp.bfloat16)
    dx_back = lax.all_to_all(dx_rows.reshape(n_exp, cap_rows, d_model), 'ep', 0, 0, tiled=True).reshape(n_slots, d_model)
    dx_pair = jnp.take(dx_back, dest_slot, axis=0).reshape(tok_dev, 2, d_model)
    d_sel = gate_val * (d_gate - jnp.sum(gate_val * d_gate, axis=1, keepdims=True))
    d_logits = jnp.sum(jnp.where(choice_hot, d_sel[:, :, None], 0.0), axis=1).astype(jnp.bfloat16)
    grad_x = (jnp.sum(dx_pair.astype(jnp.float32), axis=1) + jnp.einsum('te,me->tm', d_logits, w_gate, preferred_element_type=jnp.float32)).astype(jnp.bfloat16)
    grad_w_gate = lax.psum(jnp.einsum('tm,te->me', tokens, d_logits, preferred_element_type=jnp.float32), 'ep')
    return y_out, grad_x, g_w_in[None], g_w_out[None], grad_w_gate


def solution(mesh):
    return jax.shard_map(local_block, mesh=mesh, in_specs=(P('ep'), P('ep'), P('ep'), P(), P('ep'), P('ep')), out_specs=(P('ep'), P('ep'), P('ep'), P('ep'), P()), check_vma=False)
```

profile of v0, /device:TPU:0, one launch (start us, length us, event | category | flops | bytes accessed | tf_op | source)
XLA Modules:
  0.0 654.9 jit_solution(16002086130141430031)
XLA Ops:
  0.6 0.0 copy-start
  0.6 0.9 copy.19
  1.6 0.3 eq.39
  1.8 0.3 eq.35
  2.1 0.7 broadcast_multiply_fusion
  2.8 4.5 reduce-window.6
  7.4 0.4 slice_reduce_fusion
  7.8 0.2 reduce-window.9
  8.0 0.1 broadcast_add_fusion
  8.1 0.2 copy.21
  8.3 0.3 mul.100
  8.6 0.1 fusion.16
  8.8 8.1 %scatter_custom_fusion = s32[4096]{0:T(1024)S(1)} fusion(s32[2048]{0:T(1024)S(1)} %bitcast.79, s32[2048]{0:T(1024)S(1)} %iota.15, s32[]{:T(128)} %constant.40.clone.1), kind=kCustom, calls=%fused_computation.69 | custom fusion | bytes 16388 | tf_op jit(solution)/shard_map/scatter | solution.py:16
  16.8 0.6 fusion.23
  17.5 1.5 concatenate.6
  19.0 17.7 %gather_fusion = bf16[4096,768]{1,0:T(8,128)(2,1)} fusion(bf16[1025,768]{1,0:T(8,128)(2,1)S(1)} %concatenate.6, s32[4096]{0:T(1024)S(1)} %get-tuple-element.11), kind=kCustom, calls=%fused_computation.2 | custom fusion | bytes 12599296 | tf_op jit(solution)/shard_map/jit(_take)/gather | solution.py:32
  36.7 3.9 broadcast_select_fusion.1
  40.6 80.1 %all_to_all.20 = bf16[16,256,768]{2,1,0:T(8,128)(2,1)} all-to-all(bf16[16,256,768]{2,1,0:T(8,128)(2,1)S(1)} %broadcast_select_fusion.1), channel_id=1, replica_groups=mesh['ep'=16] {'ep'}, dimensions={0} | all-to-all | bytes 12582912 | tf_op jit(solution)/shard_map/all_to_all | solution.py:33
  120.7 42.1 %multiply_convert_fusion = (bf16[4096,3072]{1,0:T(8,128)(2,1)}, f32[4096,3072]{1,0:T(8,128)}) fusion(bf16[4096,768]{1,0:T(8,128)(2,1)} %bitcast.71, bf16[1,768,3072]{2,1,0:T(8,128)(2,1)} %param.12), kind=kOutput, calls=%fused_computation.14 | convolution fusion | flops 19440599040 | bytes 86507520 | tf_op jit(solution)/shard_map/dot_general | solution.py:34
  162.8 25.9 %convolution_convert_fusion.1 = bf16[4096,768]{1,0:T(8,128)(2,1)} fusion(bf16[4096,3072]{1,0:T(8,128)(2,1)} %get-tuple-element.12, bf16[1,3072,768]{2,1,0:T(8,128)(2,1)} %param.13), kind=kOutput, calls=%fused_computation.16 | convolution fusion | flops 19330498560 | bytes 36175872 | tf_op jit(solution)/shard_map/dot_general | solution.py:37
  188.7 3.5 all-to-all-start.1
  192.2 0.0 copy-done.6
  192.2 4.1 mul.110
  196.3 8.6 %mul.111 = f32[2048,768]{1,0:T(8,128)} reshape(f32[1024,2,768]{2,1,0:T(2,128)} %mul.110) | data formatting | bytes 12582912 | tf_op jit(solution)/shard_map/mul | solution.py:46
  205.0 0.5 fusion.31
  205.5 0.0 copy-done.9
  205.5 0.1 select_reduce_fusion.1
  205.7 67.0 %all-to-all-done.1 = bf16[16,256,768]{2,1,0:T(8,128)(2,1)} async-done(((bf16[16,256,768]{2,1,0:T(8,128)(2,1)}), bf16[16,256,768]{2,1,0:T(8,128)(2,1)}, u32[]{:S(2)}, u32[]{:S(2)}) %all-to-all-start.1) | async-done | bytes 6291488 | tf_op jit(solution)/shard_map/all_to_all | solution.py:38
  272.6 12.1 %gather_fusion.2 = bf16[2048,768]{1,0:T(8,128)(2,1)S(1)} fusion(bf16[4096,768]{1,0:T(8,128)(2,1)} %bitcast.8, s32[2048]{0:T(1024)S(1)} %broadcast_clamp_fusion.1), kind=kCustom, calls=%fused_computation.clone | custom fusion | bytes 6299648 | tf_op jit(solution)/shard_map/jit(_take)/gather | solution.py:39
  284.7 0.0 copy-done.13
  284.7 0.0 copy-done.10
  284.7 1.9 broadcast_select_fusion.2
  286.6 6.1 reshape.172
  292.7 0.0 copy-start.3
  292.7 9.5 %fusion.12 = f32[1024,1,2]{2,1,0:T(1,128)} fusion(bf16[1024,2,768]{2,1,0:T(2,128)(2,1)S(1)} %reshape.172, bf16[1024,768,1]{1,0,2:T(8,128)(2,1)} %bitcast.75), kind=kOutput, calls=%fused_computation.31 | convolution fusion | flops 3145728 | bytes 4726784 | tf_op jit(solution)/shard_map/tm,tkm->tk/dot_general | solution.py:45
  302.2 1.2 copy.24
  303.4 0.2 copy.18
  303.6 0.0 copy-start.4
  303.7 0.3 div.31
  303.9 0.5 copy-done.4
  304.4 3.2 multiply_convert_fusion.1
  307.7 0.2 concatenate.7
  307.9 17.7 %gather_fusion.1 = bf16[4096,768]{1,0:T(8,128)(2,1)} fusion(bf16[2049,768]{1,0:T(8,128)(2,1)S(1)} %concatenate.7, s32[4096]{0:T(1024)S(1)} %copy-done.12), kind=kCustom, calls=%fused_computation.3 | custom fusion | bytes 12599296 | tf_op jit(solution)/shard_map/jit(_take)/gather | solution.py:47
  325.6 6.6 %broadcast_select_fusion = bf16[16,256,768]{2,1,0:T(8,128)(2,1)} fusion(bf16[16,256,768]{2,1,0:T(8,128)(2,1)} %bitcast.70, pred[16,256]{1,0:T(8,128)(4,1)S(1)} %broadcast_in_dim.85), kind=kLoop, calls=%fused_computation.19 | loop fusion | flops 3145728 | bytes 12587008 | tf_op jit(solution)/shard_map/jit(_take)/select_n | solution.py:47
  332.3 4.5 all-to-all-start.2
  336.9 0.6 copy-done.7
  337.5 0.3 convolution_bitcast_fusion.2
  337.8 107.1 %psum.7 = f32[768,16]{0,1:T(8,128)} all-reduce(f32[768,16]{0,1:T(8,128)S(1)} %convolution_bitcast_fusion.2), channel_id=1, replica_groups=mesh['ep'=16] {'ep'}, use_global_device_ids=true, to_apply=%region_11.13 | all-reduce | flops 12288 | bytes 98304 | tf_op jit(solution)/shard_map/psum | solution.py:59
  444.9 0.0 copy-done.5
  444.9 11.2 %multiply_reduce_fusion = bf16[1024,768]{1,0:T(8,128)(2,1)} fusion(bf16[1024,2,768]{2,1,0:T(2,128)(2,1)} %copy-done.3, f32[1024,2]{1,0:T(8,128)S(1)} %copy-done.5), kind=kLoop, calls=%fused_computation.18 | loop fusion | flops 3932160 | bytes 4726784 | tf_op jit(solution)/shard_map/reduce_sum | solution.py:44
  456.1 0.0 all-to-all-done.2
  456.1 52.7 %fusion.6 = bf16[4096,3072]{1,0:T(8,128)(2,1)} fusion(f32[4096,3072]{1,0:T(8,128)} %get-tuple-element.13, bf16[4096,768]{1,0:T(8,128)(2,1)} %bitcast.10, bf16[1,3072,768]{2,1,0:T(8,128)(2,1)} %param.13), kind=kOutput, calls=%fused_computation.13 | convolution fusion | flops 19579011072 | bytes 86507520 | tf_op jit(solution)/shard_map/rm,hm->rh/dot_general | solution.py:50
  508.9 25.6 %convolution_convert_fusion = bf16[4096,768]{1,0:T(8,128)(2,1)} fusion(bf16[4096,3072]{1,0:T(8,128)(2,1)} %fusion.6, bf16[1,768,3072]{2,1,0:T(8,128)(2,1)} %param.12), kind=kOutput, calls=%fused_computation.15 | convolution fusion | flops 19330498560 | bytes 36175872 | tf_op jit(solution)/shard_map/rh,mh->rm/dot_general | solution.py:53
  534.5 4.1 all-to-all-start.3
  538.6 26.6 %convolution_bitcast_fusion.1 = f32[1,768,3072]{2,1,0:T(8,128)} fusion(bf16[4096,768]{1,0:T(8,128)(2,1)} %bitcast.72, bf16[4096,3072]{1,0:T(8,128)(2,1)} %fusion.6), kind=kOutput, calls=%fused_computation.22 | convolution fusion | flops 19327352832 | bytes 40894464 | tf_op jit(solution)/shard_map/rm,rh->mh/dot_general | solution.py:52
  565.2 26.6 %convolution_bitcast_fusion = f32[1,3072,768]{2,1,0:T(8,128)} fusion(bf16[4096,3072]{1,0:T(8,128)(2,1)} %get-tuple-element.12, bf16[4096,768]{1,0:T(8,128)(2,1)} %bitcast.10), kind=kOutput, calls=%fused_computation.21 | convolution fusion | flops 19327352832 | bytes 40894464 | tf_op jit(solution)/shard_map/rh,rm->hm/dot_general | solution.py:49
  591.8 27.2 %all-to-all-done.3 = bf16[16,256,768]{2,1,0:T(8,128)(2,1)} async-done(((bf16[16,256,768]{2,1,0:T(8,128)(2,1)}), bf16[16,256,768]{2,1,0:T(8,128)(2,1)}, u32[]{:S(2)}, u32[]{:S(2)}) %all-to-all-start.3) | async-done | bytes 6291488 | tf_op jit(solution)/shard_map/all_to_all | solution.py:54
  619.0 0.0 copy-done.11
  619.0 12.1 %gather_fusion.3 = bf16[2048,768]{1,0:T(8,128)(2,1)S(1)} fusion(bf16[4096,768]{1,0:T(8,128)(2,1)} %bitcast.12, s32[2048]{0:T(1024)S(1)} %copy-done.11), kind=kCustom, calls=%fused_computation.1.clone | custom fusion | bytes 6299648 | tf_op jit(solution)/shard_map/jit(_take)/gather | solution.py:55
  631.1 0.0 copy-done.14
  631.1 3.0 select_convert_fusion
  634.0 8.4 %reshape.176 = f32[1024,2,768]{2,1,0:T(2,128)} reshape(f32[2048,768]{1,0:T(8,128)} %select_convert_fusion) | data formatting | bytes 12582912 | tf_op jit(solution)/shard_map/convert_element_type | solution.py:58
  642.4 10.3 %reduce_sum.70 = f32[1024,768]{1,0:T(8,128)S(1)} reduce(f32[1024,2,768]{2,1,0:T(2,128)} %reshape.176, f32[]{:T(128)} %constant.38.clone.1), dimensions={1}, to_apply=%region_8.10 | reduce | flops 786432 | bytes 9437188 | tf_op jit(solution)/shard_map/reduce_sum | solution.py:58
  652.7 1.8 add_convert_fusion
  (31 shorter events, 0.2 us)
Async XLA Ops:
  0.6 204.3 %copy-start = (bf16[768,16]{0,1:T(8,128)(2,1)S(1)}, bf16[768,16]{0,1:T(8,128)(2,1)}, u32[]{:S(2)}) copy-start(bf16[768,16]{0,1:T(8,128)(2,1)} %param.11) | copy-start | bytes 73732
  188.7 3.5 copy-start.6
  188.7 83.9 %all-to-all-start.1 = ((bf16[16,256,768]{2,1,0:T(8,128)(2,1)}), bf16[16,256,768]{2,1,0:T(8,128)(2,1)}, u32[]{:S(2)}, u32[]{:S(2)}) async-start(bf16[16,256,768]{2,1,0:T(8,128)(2,1)} %bitcast.73), calls=%async_computation.1 | async-start | bytes 12582912 | tf_op jit(solution)/shard_map/all_to_all | solution.py:38
  196.3 8.6 %copy-start.1 = (bf16[1024,768]{1,0:T(8,128)(2,1)S(1)}, bf16[1024,768]{1,0:T(8,128)(2,1)}, u32[]{:S(2)}) copy-start(bf16[1024,768]{1,0:T(8,128)(2,1)} %param.8) | copy-start | bytes 4718596
  196.3 9.2 %copy-start.9 = (s32[1024,2]{0,1:T(2,128)S(1)}, s32[1024,2]{0,1:T(2,128)}, u32[]{:S(2)}) copy-start(s32[1024,2]{0,1:T(2,128)} %param.10) | copy-start | bytes 24580
  205.6 79.1 %copy-start.13 = (pred[2048]{0:T(1024)(128)(4,1)}, pred[2048]{0:T(1024)(128)(4,1)S(1)}, u32[]{:S(2)}) copy-start(pred[2048]{0:T(1024)(128)(4,1)S(1)} %compare_and_fusion.2) | copy-start | bytes 6148
  205.7 79.1 %copy-start.10 = (s32[2048]{0:T(1024)}, s32[2048]{0:T(1024)S(1)}, u32[]{:S(2)}) copy-start(s32[2048]{0:T(1024)S(1)} %broadcast_clamp_fusion.1) | copy-start | bytes 24580
  292.7 9.5 %copy-start.3 = (bf16[1024,2,768]{2,1,0:T(2,128)(2,1)}, bf16[1024,2,768]{2,1,0:T(2,128)(2,1)S(1)}, u32[]{:S(2)}) copy-start(bf16[1024,2,768]{2,1,0:T(2,128)(2,1)S(1)} %reshape.172) | copy-start | bytes 9437188
  303.6 0.8 copy-start.4
  304.4 3.4 copy-start.12
  332.3 5.2 copy-start.2
  332.3 112.7 %copy-start.5 = (f32[1024,2]{1,0:T(8,128)S(1)}, f32[1024,2]{1,0:T(8,128)}, u32[]{:S(2)}) copy-start(f32[1024,2]{1,0:T(8,128)} %copy-done.4) | copy-start | bytes 24580
  332.3 123.9 %all-to-all-start.2 = ((bf16[16,256,768]{2,1,0:T(8,128)(2,1)}), bf16[16,256,768]{2,1,0:T(8,128)(2,1)}, u32[]{:S(2)}, u32[]{:S(2)}) async-start(bf16[16,256,768]{2,1,0:T(8,128)(2,1)} %broadcast_select_fusion), calls=%async_computation.2 | async-start | bytes 12582912 | tf_op jit(solution)/shard_map/all_to_all | solution.py:48
  336.9 0.6 copy-start.7
  534.5 84.5 %all-to-all-start.3 = ((bf16[16,256,768]{2,1,0:T(8,128)(2,1)}), bf16[16,256,768]{2,1,0:T(8,128)(2,1)}, u32[]{:S(2)}, u32[]{:S(2)}) async-start(bf16[16,256,768]{2,1,0:T(8,128)(2,1)} %bitcast.74), calls=%async_computation.3 | async-start | bytes 12582912 | tf_op jit(solution)/shard_map/all_to_all | solution.py:54
  565.2 53.8 %copy-start.11 = (s32[2048]{0:T(1024)S(1)}, s32[2048]{0:T(1024)}, u32[]{:S(2)}) copy-start(s32[2048]{0:T(1024)} %copy-done.10) | copy-start | bytes 24580
  619.0 12.1 %copy-start.14 = (pred[2048]{0:T(1024)(128)(4,1)S(1)}, pred[2048]{0:T(1024)(128)(4,1)}, u32[]{:S(2)}) copy-start(pred[2048]{0:T(1024)(128)(4,1)} %copy-done.13) | copy-start | bytes 6148
  642.4 10.3 %copy-start.8 = (bf16[1024,16]{0,1:T(8,128)(2,1)S(1)}, bf16[1024,16]{0,1:T(8,128)(2,1)}, u32[]{:S(2)}) copy-start(bf16[1024,16]{0,1:T(8,128)(2,1)} %copy-done.7) | copy-start | bytes 98308
where the time goes:
time: 660 us; the launch traced here: 655 us
  matrix products  212 us (32%)
  blocking collectives  187 us (28%)
  local copies, waits for them, and re-layouts  102 us (15%)
  waiting for transfers between devices  94.1 us (14%)
  other arithmetic  46.5 us (7%)
  starting transfers between devices  12.2 us (2%)
    psum x1, blocking collectives, local_block(): lax.psum(jnp.einsum('tm,te->me', tokens, d_logits, preferred_element_type...  107 us
    all_to_all x1, blocking collectives, local_block(): lax.all_to_all(send_x.reshape(n_exp, cap_rows, d_model), 'ep', 0, 0, tile...  80.1 us
    all_to_all x1, waiting for transfers between devices, local_block(): lax.all_to_all(y_rows.reshape(n_exp, cap_rows, d_model), 'ep', 0, 0, tile...  67 us
    dot_general x1, matrix products, local_block(): jnp.einsum('rm,hm->rh', recv_dy, w_two, preferred_element_type=jnp.float32)  52.7 us
    dot_general x1, matrix products, local_block(): a_pre = jnp.dot(recv_x, w_one, preferred_element_type=jnp.float32)  42.1 us
    all_to_all x1, waiting for transfers between devices, local_block(): lax.all_to_all(dx_rows.reshape(n_exp, cap_rows, d_model), 'ep', 0, 0, til...  27.2 us
    dot_general x1, matrix products, local_block(): jnp.einsum('rm,rh->mh', recv_x, d_pre, preferred_element_type=jnp.float32)  26.6 us
    dot_general x1, matrix products, local_block(): jnp.einsum('rh,rm->hm', hid_b, recv_dy, preferred_element_type=jnp.float32)  26.6 us
  transfers between devices with their start and end apart: 3, of which 2 were waited for; matrix products, arithmetic and copies ran while one was open for 12% of the time, Pallas kernels for 0%

commit v1 on v0

v1 whole, which is shorter than its diff:
```python
import functools

import jax
import jax.numpy as jnp
from jax import lax
from jax.experimental import pallas as pl
from jax.experimental.pallas import tpu as pltpu
from jax.sharding import PartitionSpec as P

BASE = 104
EXTRA = 80
FULL = 256
F32 = jnp.float32
BF16 = jnp.bfloat16


def slot_of(ids, rank, base, extra):
    if not extra:
        return ids * base + rank
    block = base + extra
    over = rank - base
    second = (over >= extra).astype(jnp.int32)
    spill = ((ids & -2) + second) * block + base + over - second * extra
    return jnp.where(rank < base, ids * block + rank, spill)


def softmax_pair(l0, l1):
    top = jnp.maximum(l0, l1)
    e0 = jnp.exp(l0 - top)
    e1 = jnp.exp(l1 - top)
    tot = e0 + e1
    return e0 / tot, e1 / tot


def dispatch_kernel(base, extra, x_ref, do_ref, ids_ref, idst_ref, wg_ref, sx_ref, sdy_ref, slot_ref, gate_ref, slott_ref, gatet_ref):
    n_tok = x_ref.shape[0]
    n_exp = wg_ref.shape[1]
    step = pl.program_id(0)
    rows = base + extra

    @pl.when(step == 0)
    def _():
        r_i = lax.broadcasted_iota(jnp.int32, (n_tok, n_tok), 0)
        c_i = lax.broadcasted_iota(jnp.int32, (n_tok, n_tok), 1)
        e_col = lax.broadcasted_iota(jnp.int32, (n_tok, n_exp), 1)
        id0, id1 = ids_ref[:, 0:1], ids_ref[:, 1:2]
        h0, h1 = id0 == e_col, id1 == e_col
        lower = jnp.where(c_i < r_i, 1.0, 0.0).astype(BF16)
        named = jnp.where(h0 | h1, 1.0, 0.0).astype(BF16)
        before = jnp.dot(lower, named, preferred_element_type=F32)
        logits = jnp.dot(x_ref[...], wg_ref[...], preferred_element_type=F32)
        pick = lambda hot, val: jnp.sum(jnp.where(hot, val, 0.0), axis=1, keepdims=True)
        slot_ref[:, 0:1] = slot_of(id0, pick(h0, before).astype(jnp.int32), base, extra)
        slot_ref[:, 1:2] = slot_of(id1, pick(h1, before).astype(jnp.int32), base, extra)
        g0, g1 = softmax_pair(pick(h0, logits), pick(h1, logits))
        gate_ref[:, 0:1] = g0
        gate_ref[:, 1:2] = g1
        e_row = lax.broadcasted_iota(jnp.int32, (n_exp, n_tok), 0)
        it0, it1 = idst_ref[0:1, :], idst_ref[1:2, :]
        t0, t1 = it0 == e_row, it1 == e_row
        upper = jnp.where(r_i < c_i, 1.0, 0.0).astype(BF16)
        named_t = jnp.where(t0 | t1, 1.0, 0.0).astype(BF16)
        before_t = jnp.dot(named_t, upper, preferred_element_type=F32)
        logits_t = lax.dot_general(wg_ref[...], x_ref[...], (((0,), (1,)), ((), ())), preferred_element_type=F32)
        pick_t = lambda hot, val: jnp.sum(jnp.where(hot, val, 0.0), axis=0, keepdims=True)
        slott_ref[0:1, :] = slot_of(it0, pick_t(t0, before_t).astype(jnp.int32), base, extra)
        slott_ref[1:2, :] = slot_of(it1, pick_t(t1, before_t).astype(jnp.int32), base, extra)
        g0t, g1t = softmax_pair(pick_t(t0, logits_t), pick_t(t1, logits_t))
        gatet_ref[0:1, :] = g0t
        gatet_ref[1:2, :] = g1t

    row = step * rows + lax.broadcasted_iota(jnp.int32, (rows, n_tok), 0)
    d0 = slott_ref[0:1, :] == row
    d1 = slott_ref[1:2, :] == row
    sel = jnp.where(d0 | d1, 1.0, 0.0).astype(BF16)
    g_row = jnp.sum(jnp.where(d0, gatet_ref[0:1, :], 0.0) + jnp.where(d1, gatet_ref[1:2, :], 0.0), axis=1, keepdims=True)
    sx_ref[0] = jnp.dot(sel, x_ref[...], preferred_element_type=F32).astype(BF16)
    sdy_ref[0] = (g_row * jnp.dot(sel, do_ref[...], preferred_element_type=F32)).astype(BF16)


def dispatch(tokens, grad_out, ids, w_gate, base, extra):
    n_tok, d_model = tokens.shape
    n_exp = w_gate.shape[1]
    rows = base + extra
    whole = lambda shape: pl.BlockSpec(shape, lambda i: (0,) * len(shape))
    block = pl.BlockSpec((1, rows, d_model), lambda i: (i, 0, 0))
    send = jax.ShapeDtypeStruct((n_exp, rows, d_model), BF16)
    return pl.pallas_call(
        functools.partial(dispatch_kernel, base, extra),
        grid=(n_exp,),
        in_specs=[whole((n_tok, d_model)), whole((n_tok, d_model)), whole((n_tok, 2)), whole((2, n_tok)), whole((d_model, n_exp))],
        out_specs=[block, block, whole((n_tok, 2)), whole((n_tok, 2))],
        out_shape=[send, send, jax.ShapeDtypeStruct((n_tok, 2), jnp.int32), jax.ShapeDtypeStruct((n_tok, 2), F32)],
        scratch_shapes=[pltpu.VMEM((2, n_tok), jnp.int32), pltpu.VMEM((2, n_tok), F32)],
        compiler_params=pltpu.CompilerParams(vmem_limit_bytes=56 * 2 ** 20),
        cost_estimate=pl.CostEstimate(flops=4 * n_exp * rows * n_tok * d_model, bytes_accessed=4 * n_exp * rows * d_model, transcendentals=0),
        name='dispatch',
    )(tokens, grad_out, ids, ids.T, w_gate)


def gather_y_kernel(y_ref, do_ref, x_ref, ids_ref, slot_ref, gate_ref, out_ref, dl_ref, gw_ref):
    n_tile = do_ref.shape[0]
    n_exp = dl_ref.shape[1]
    col = lax.broadcasted_iota(jnp.int32, (n_tile, y_ref.shape[0]), 1)
    s0 = jnp.where(slot_ref[:, 0:1] == col, 1.0, 0.0).astype(BF16)
    s1 = jnp.where(slot_ref[:, 1:2] == col, 1.0, 0.0).astype(BF16)
    y0 = jnp.dot(s0, y_ref[...], preferred_element_type=F32)
    y1 = jnp.dot(s1, y_ref[...], preferred_element_type=F32)
    g0, g1 = gate_ref[:, 0:1], gate_ref[:, 1:2]
    out_ref[...] = (g0 * y0 + g1 * y1).astype(BF16)
    do = do_ref[...].astype(F32)
    dg0 = jnp.sum(do * y0, axis=1, keepdims=True)
    dg1 = jnp.sum(do * y1, axis=1, keepdims=True)
    mean = g0 * dg0 + g1 * dg1
    e_col = lax.broadcasted_iota(jnp.int32, (n_tile, n_exp), 1)
    dl = jnp.where(ids_ref[:, 0:1] == e_col, g0 * (dg0 - mean), 0.0) + jnp.where(ids_ref[:, 1:2] == e_col, g1 * (dg1 - mean), 0.0)
    dl = dl.astype(BF16)
    dl_ref[...] = dl

    @pl.when(pl.program_id(0) == 0)
    def _():
        gw_ref[...] = jnp.zeros_like(gw_ref)

    gw_ref[...] += lax.dot_general(x_ref[...], dl, (((0,), (0,)), ((), ())), preferred_element_type=F32)


def gather_y(y_back, grad_out, tokens, ids, slots, gates, n_exp):
    n_tok, d_model = tokens.shape
    n_slot = y_back.shape[0]
    tile = 256
    per = lambda width: pl.BlockSpec((tile, width), lambda i: (i, 0))
    return pl.pallas_call(
        gather_y_kernel,
        grid=(n_tok // tile,),
        in_specs=[pl.BlockSpec((n_slot, d_model), lambda i: (0, 0)), per(d_model), per(d_model), per(2), per(2), per(2)],
        out_specs=[per(d_model), per(n_exp), pl.BlockSpec((d_model, n_exp), lambda i: (0, 0))],
        out_shape=[jax.ShapeDtypeStruct((n_tok, d_model), BF16), jax.ShapeDtypeStruct((n_tok, n_exp), BF16), jax.ShapeDtypeStruct((d_model, n_exp), F32)],
        compiler_params=pltpu.CompilerParams(vmem_limit_bytes=56 * 2 ** 20),
        cost_estimate=pl.CostEstimate(flops=4 * n_slot * n_tok * d_model, bytes_accessed=2 * n_slot * d_model, transcendentals=0),
        name='gather_y',
    )(y_back, grad_out, tokens, ids, slots, gates)


def gather_dx_kernel(dx_ref, dl_ref, wg_ref, slot_ref, out_ref):
    col = lax.broadcasted_iota(jnp.int32, (out_ref.shape[0], dx_ref.shape[0]), 1)
    sel = jnp.where((slot_ref[:, 0:1] == col) | (slot_ref[:, 1:2] == col), 1.0, 0.0).astype(BF16)
    tot = jnp.dot(sel, dx_ref[...], preferred_element_type=F32)
    tot += lax.dot_general(dl_ref[...], wg_ref[...], (((1,), (1,)), ((), ())), preferred_element_type=F32)
    out_ref[...] = tot.astype(BF16)


def gather_dx(dx_back, d_logits, w_gate, slots):
    n_tok, n_exp = d_logits.shape
    n_slot, d_model = dx_back.shape
    tile = 256
    per = lambda width: pl.BlockSpec((tile, width), lambda i: (i, 0))
    return pl.pallas_call(
        gather_dx_kernel,
        grid=(n_tok // tile,),
        in_specs=[pl.BlockSpec((n_slot, d_model), lambda i: (0, 0)), per(n_exp), pl.BlockSpec((d_model, n_exp), lambda i: (0, 0)), per(2)],
        out_specs=per(d_model),
        out_shape=jax.ShapeDtypeStruct((n_tok, d_model), BF16),
        compiler_params=pltpu.CompilerParams(vmem_limit_bytes=56 * 2 ** 20),
        cost_estimate=pl.CostEstimate(flops=2 * n_slot * n_tok * d_model, bytes_accessed=2 * n_slot * d_model, transcendentals=0),
        name='gather_dx',
    )(dx_back, d_logits, w_gate, slots)


def swap(value, n_dev):
    return lax.ppermute(value, 'ep', [(d, d ^ 1) for d in range(n_dev)])


def exchange(value):
    return lax.all_to_all(value, 'ep', 0, 0, tiled=True)


def expert_fwd(rows, w_one, w_two):
    a_pre = jnp.dot(rows, w_one, preferred_element_type=F32)
    hidden, gelu_vjp = jax.vjp(jax.nn.gelu, a_pre)
    hid_b = hidden.astype(BF16)
    y_rows = jnp.dot(hid_b, w_two, preferred_element_type=F32).astype(BF16)
    return hid_b, gelu_vjp, y_rows


def expert_bwd(dy_rows, gelu_vjp, w_one, w_two):
    d_hid = jnp.einsum('rm,hm->rh', dy_rows, w_two, preferred_element_type=F32)
    d_pre = gelu_vjp(d_hid)[0].astype(BF16)
    return d_pre, jnp.einsum('rh,mh->rm', d_pre, w_one, preferred_element_type=F32).astype(BF16)


def weight_grads(rows, hid_b, dy_rows, d_pre):
    g_two = jnp.einsum('rh,rm->hm', hid_b, dy_rows, preferred_element_type=F32)
    g_one = jnp.einsum('rm,rh->mh', rows, d_pre, preferred_element_type=F32)
    return g_one, g_two


def run_path(base, extra, tokens, grad_out, ids, w_gate, w_one, w_two, mine):
    n_exp = w_gate.shape[1]
    d_model = tokens.shape[1]
    rows = base + extra
    send_x, send_dy, slots, gates = dispatch(tokens, grad_out, ids, w_gate, base, extra)
    recv_x = exchange(send_x)
    recv_dy = exchange(send_dy)
    first = lambda v: v[:, :base].reshape(n_exp * base, d_model)
    x_b, dy_b = first(recv_x), first(recv_dy)
    hid_b, vjp_b, y_b = expert_fwd(x_b, w_one, w_two)
    if extra:
        last = lambda v: v[:, base:].reshape(n_exp * extra, d_model)
        x_e, dy_e = last(recv_x), last(recv_dy)
        hot_one = jnp.where(mine, w_one, swap(w_one, n_exp))
        hot_two = jnp.where(mine, w_two, swap(w_two, n_exp))
        hid_e, vjp_e, y_e = expert_fwd(x_e, hot_one, hot_two)
        y_rows = jnp.concatenate([y_b.reshape(n_exp, base, d_model), y_e.reshape(n_exp, extra, d_model)], axis=1)
    else:
        y_rows = y_b.reshape(n_exp, base, d_model)
    y_back = exchange(y_rows).reshape(n_exp * rows, d_model)
    dp_b, dx_b = expert_bwd(dy_b, vjp_b, w_one, w_two)
    if extra:
        dp_e, dx_e = expert_bwd(dy_e, vjp_e, hot_one, hot_two)
        dx_rows = jnp.concatenate([dx_b.reshape(n_exp, base, d_model), dx_e.reshape(n_exp, extra, d_model)], axis=1)
    else:
        dx_rows = dx_b.reshape(n_exp, base, d_model)
    dx_back = exchange(dx_rows).reshape(n_exp * rows, d_model)
    g_one, g_two = weight_grads(x_b, hid_b, dy_b, dp_b)
    if extra:
        e_one, e_two = weight_grads(x_e, hid_e, dy_e, dp_e)
        keep = jnp.where(mine, 1.0, 0.0)
        g_one = g_one + keep * (e_one + swap(e_one, n_exp))
        g_two = g_two + keep * (e_two + swap(e_two, n_exp))
    y_out, d_logits, gw_part = gather_y(y_back, grad_out, tokens, ids, slots, gates, n_exp)
    grad_w_gate = lax.psum(gw_part, 'ep')
    grad_x = gather_dx(dx_back, d_logits, w_gate, slots)
    return y_out, grad_x, g_one, g_two, grad_w_gate


def local_block(tokens, grad_out, expert_ids, w_gate, w_in, w_out):
    n_exp = w_gate.shape[1]
    me = lax.axis_index('ep')
    counts = jnp.sum((expert_ids.reshape(-1)[:, None] == jnp.arange(n_exp)[None, :]).astype(jnp.int32), axis=0)
    most = lax.pmax(counts, 'ep')
    over = most > BASE
    mine = over[me]
    both = jnp.any(over.reshape(n_exp // 2, 2).all(axis=1))
    args = (tokens, grad_out, expert_ids, w_gate, w_in[0], w_out[0], mine)
    y_out, grad_x, g_one, g_two, g_gate = lax.cond(both, functools.partial(run_path, FULL, 0), functools.partial(run_path, BASE, EXTRA), *args)
    return y_out, grad_x, g_one[None], g_two[None], g_gate


def solution(mesh):
    return jax.shard_map(local_block, mesh=mesh, in_specs=(P('ep'), P('ep'), P('ep'), P(), P('ep'), P('ep')), out_specs=(P('ep'), P('ep'), P('ep'), P('ep'), P()), check_vma=False)
```

time: 660 us -> 476 us (0.72); the launches traced: 655 us -> 485 us
  local copies, waits for them, and re-layouts: 102 us -> 15.4 us
  blocking collectives: 187 us -> 131 us
  Pallas kernels: 0 us -> 47 us
  other arithmetic: 46.5 us -> 5.89 us
  matrix products: 212 us -> 184 us
  waiting for transfers between devices: 94.1 us -> 76.1 us
  loops' own time: 0 us -> 9.9 us
    psum x1, blocking collectives: 107 us -> 37 us  [run_path(): grad_w_gate = lax.psum(gw_part, 'ep')]
    gather x4 -> x0, local copies, waits for them, and re-layouts: 59.6 us -> none  [the longest x1 17.7 us: local_block(): jnp.take(x_table, jnp.where(src_choice < n_choice, src_choice // 2, tok_d...]
    pallas_call x0 -> x3, Pallas kernels: none -> 47 us  [the longest x1 19.9 us: dispatch(): pl.pallas_call(functools.partial(dispatch_kernel, base, extra), grid=(n_e...]
    pmax x0 -> x1, blocking collectives: none -> 34.7 us  [local_block(): most = lax.pmax(counts, 'ep')]
    dot_general x10 -> x12, matrix products: 212 us -> 184 us  [the longest x2 45.9 us: expert_bwd(): d_hid = jnp.einsum('rm,hm->rh', dy_rows, w_two, preferred_element_type=F32)]
    reduce_sum x7 -> x1, other arithmetic: 21.7 us -> 0.13 us  [local_block(): jnp.sum((expert_ids.reshape(-1)[:, None] == jnp.arange(n_exp)[None, :]).a...]
    all_to_all x1, blocking collectives: 80.1 us -> 59.8 us  [exchange(): return lax.all_to_all(value, 'ep', 0, 0, tiled=True)]
    all_to_all x3, waiting for transfers between devices: 94.1 us -> 76.1 us  [exchange(): return lax.all_to_all(value, 'ep', 0, 0, tiled=True)]
  transfers between devices with their start and end apart: 3 -> 7, of which waited for: 2 -> 3; matrix products, arithmetic and copies ran while one was open for 12% -> 38% of each run, Pallas kernels for 0% -> 6%
where the time goes in v1:
time: 476 us; the launch traced here: 485 us
  matrix products  184 us (39%)
  blocking collectives  131 us (28%)
  waiting for transfers between devices  76.1 us (16%)
  Pallas kernels  47 us (10%)
  local copies, waits for them, and re-layouts  15.4 us (3%)
  starting transfers between devices  13.8 us (3%)
  loops' own time  9.9 us (2%)
  other arithmetic  5.89 us (1%)
    all_to_all x3, waiting for transfers between devices, exchange(): return lax.all_to_all(value, 'ep', 0, 0, tiled=True)  76.1 us
    all_to_all x1, blocking collectives, exchange(): return lax.all_to_all(value, 'ep', 0, 0, tiled=True)  59.8 us
    dot_general x2, matrix products, expert_bwd(): d_hid = jnp.einsum('rm,hm->rh', dy_rows, w_two, preferred_element_type=F32)  45.9 us
    psum x1, blocking collectives, run_path(): grad_w_gate = lax.psum(gw_part, 'ep')  37 us
    pmax x1, blocking collectives, local_block(): most = lax.pmax(counts, 'ep')  34.7 us
    dot_general x2, matrix products, weight_grads(): g_two = jnp.einsum('rh,rm->hm', hid_b, dy_rows, preferred_element_type=F32)  32.8 us
    dot_general x2, matrix products, expert_fwd(): a_pre = jnp.dot(rows, w_one, preferred_element_type=F32)  31.8 us
    dot_general x2, matrix products, weight_grads(): g_one = jnp.einsum('rm,rh->mh', rows, d_pre, preferred_element_type=F32)  27 us
  transfers between devices with their start and end apart: 7, of which 3 were waited for; matrix products, arithmetic and copies ran while one was open for 38% of the time, Pallas kernels for 6%

profile of v1, /device:TPU:0, one launch (start us, length us, event | category | flops | bytes accessed | tf_op | source)
XLA Modules:
  0.0 485.4 jit_solution(11934544905928805938)
XLA Ops:
  0.6 0.9 copy.28
  1.6 0.3 eq.15
  1.8 0.1 convert_reduce_fusion
  2.0 34.7 %pmax.7 = s32[16]{0:T(128)S(1)} all-reduce(s32[16]{0:T(128)S(1)} %convert_reduce_fusion), channel_id=1, replica_groups=mesh['ep'=16] {'ep'}, use_global_device_ids=true, to_apply=%region_1.0 | all-reduce | flops 16 | bytes 128 | tf_op jit(solution)/shard_map/pmax | solution.py:240
  36.7 0.1 reshape.62
  36.8 0.1 reduce_and.9
  36.9 0.6 reduce_or.9
  38.2 409.1 %conditional.1 = (bf16[1024,768]{1,0:T(8,128)(2,1)}, f32[1,768,3072]{2,1,0:T(8,128)}, f32[1,3072,768]{2,1,0:T(8,128)}, (bf16[1024,768]{1,0:T(8,128)(2,1)}, bf16[1024,16]{1,0:T(8,128)(2,1)}, f32[768,16]{1,0:T(8,128)})) conditional(s32[]{:T(128)} %convert_element_type.43, (s32[1024,2]{0,1:T(2,128)}, bf16[1024,768]{1,0:T(8,128)(2,1)}, ...), branch_computations={%region_4.6_spmd, %region_6.8_spmd} | conditional | flops 148547567616 | bytes 735970048 | solution.py:245
  38.2 1.6 copy.30.wg_ref
  39.8 1.7 copy.29.ids_ref
  41.5 19.9 %dispatch.2 = (bf16[16,184,768]{2,1,0:T(8,128)(2,1)}, bf16[16,184,768]{2,1,0:T(8,128)(2,1)}, s32[1024,2]{1,0:T(8,128)}, f32[1024,2]{1,0:T(8,128)}) custom-call(bf16[1024,768]{1,0:T(8,128)(2,1)} %get-tuple-element.28.x_ref, bf16[1024,768]{1,0:T(8,128)(2,1)} %get-tuple-element.29.do_ref, s32[1024,2]{1,0:T(8,128)} %copy.29.ids_ref, s32[2,1024]{1,0:T(2,128)} %bitcast.79, ...), custom_call_target="tpu_custom_call" | custom-call | flops 9261023232 | bytes 9043968 | tf_op jit(solution)/shard_map/cond/branch_0_fun/dispatch/pallas_call | solution.py:88
  61.4 59.8 %all_to_all.32 = bf16[16,184,768]{2,1,0:T(8,128)(2,1)} all-to-all(bf16[16,184,768]{2,1,0:T(8,128)(2,1)} %get-tuple-element.32), channel_id=1, replica_groups=mesh['ep'=16] {'ep'}, dimensions={0} | all-to-all | bytes 9043968 | tf_op jit(solution)/shard_map/cond/branch_0_fun/all_to_all | solution.py:174
  121.2 4.5 all-to-all-start.2
  125.7 0.5 collective-permute-start.1
  126.2 0.1 collective-permute-start
  126.2 0.6 dynamic_slice.4
  126.8 1.9 slice.13
  128.7 1.4 copy-done
  130.2 18.9 %multiply_convert_fusion = (bf16[1664,3072]{1,0:T(8,128)(2,1)}, f32[1664,3072]{1,0:T(8,128)}) fusion(bf16[1664,768]{1,0:T(8,128)(2,1)S(1)} %bitcast.63, bf16[768,3072]{1,0:T(8,128)(2,1)} %get-tuple-element.33), kind=kOutput, calls=%fused_computation.11 | convolution fusion | flops 7897743360 | bytes 37945344 | tf_op jit(solution)/shard_map/cond/branch_0_fun/dot_general | solution.py:178
  149.1 34.8 %all-to-all-done.2 = bf16[16,184,768]{2,1,0:T(8,128)(2,1)} async-done(((bf16[16,184,768]{2,1,0:T(8,128)(2,1)}), bf16[16,184,768]{2,1,0:T(8,128)(2,1)}, u32[]{:S(2)}, u32[]{:S(2)}) %all-to-all-start.2) | async-done | bytes 4522016 | tf_op jit(solution)/shard_map/cond/branch_0_fun/all_to_all | solution.py:174
  183.9 2.0 slice.12
  185.9 0.0 slice-start.11
  185.9 0.0 slice-start.7
  186.0 24.4 %fusion.6 = bf16[1664,3072]{1,0:T(8,128)(2,1)} fusion(f32[1664,3072]{1,0:T(8,128)} %get-tuple-element.156, bf16[1664,768]{1,0:T(8,128)(2,1)S(1)} %bitcast.69, bf16[3072,768]{1,0:T(8,128)(2,1)} %get-tuple-element.34), kind=kOutput, calls=%fused_computation.10 | convolution fusion | flops 7953973248 | bytes 37945344 | tf_op jit(solution)/shard_map/cond/branch_0_fun/rm,hm->rh/dot_general | solution.py:186
  210.4 0.0 slice-done.10
  210.4 10.8 %convolution_convert_fusion.3 = bf16[1664,768]{1,0:T(8,128)(2,1)S(1)} fusion(bf16[1664,3072]{1,0:T(8,128)(2,1)} %get-tuple-element.155, bf16[3072,768]{1,0:T(8,128)(2,1)S(1)} %bitcast.90), kind=kOutput, calls=%fused_computation.29 | convolution fusion | flops 7853015040 | bytes 17498112 | tf_op jit(solution)/shard_map/cond/branch_0_fun/dot_general | solution.py:181
  221.2 1.7 slice.14
  222.9 0.0 copy-start.5
  222.9 2.4 slice.15
  225.3 0.0 collective-permute-done
  225.3 12.9 %fusion.14 = f32[1280,3072]{1,0:T(8,128)} fusion(bf16[1280,768]{1,0:T(8,128)(2,1)S(1)} %bitcast.73, bf16[768,3072]{1,0:T(8,128)(2,1)S(1)} %bitcast.84, bf16[768,3072]{1,0:T(8,128)(2,1)} %collective-permute-done, pred[]{:T(512)} %bitcast.4), kind=kOutput, calls=%fused_computation.30 | convolution fusion | flops 6042157056 | bytes 27131904 | tf_op jit(solution)/shard_map/cond/branch_0_fun/dot_general | solution.py:178
  238.3 0.0 copy-done.5
  238.3 14.0 %fusion.15 = f32[3072,768]{1,0:T(8,128)} fusion(bf16[1280,768]{1,0:T(8,128)(2,1)S(1)} %bitcast.75, f32[1280,3072]{1,0:T(8,128)} %fusion.14), kind=kOutput, calls=%fused_computation.31 | convolution fusion | flops 6075187200 | bytes 27131904 | tf_op jit(solution)/shard_map/cond/branch_0_fun/rh,rm->hm/dot_general | solution.py:192
  252.3 0.3 collective-permute-start.3
  252.6 0.0 collective-permute-done.1
  252.6 15.0 %convolution_convert_fusion.2 = bf16[1280,768]{1,0:T(8,128)(2,1)S(1)} fusion(bf16[3072,768]{1,0:T(8,128)(2,1)S(1)} %bitcast.90, bf16[3072,768]{1,0:T(8,128)(2,1)} %collective-permute-done.1, pred[]{:T(512)} %bitcast.4, f32[1280,3072]{1,0:T(8,128)} %fusion.14), kind=kOutput, calls=%fused_computation.28 | convolution fusion | flops 6078529536 | bytes 27131904 | tf_op jit(solution)/shard_map/cond/branch_0_fun/dot_general | solution.py:181
  267.6 2.4 pad_maximum_fusion.1
  270.1 3.9 all-to-all-start.1
  274.0 0.0 slice-start.1
  274.0 0.0 slice-start.2
  274.0 21.5 %fusion.13 = bf16[1280,3072]{1,0:T(8,128)(2,1)} fusion(f32[1280,3072]{1,0:T(8,128)} %fusion.14, bf16[1280,768]{1,0:T(8,128)(2,1)} %bitcast.76, bf16[3072,768]{1,0:T(8,128)(2,1)} %get-tuple-element.34, bf16[3072,768]{1,0:T(8,128)(2,1)} %collective-permute-done.1, pred[]{:T(512)} %bitcast.4), kind=kOutput, calls=%fused_computation.18 | convolution fusion | flops 6120800256 | bytes 34996224 | tf_op jit(solution)/shard_map/cond/branch_0_fun/rm,hm->rh/dot_general | solution.py:186
  295.5 12.2 %fusion.23 = f32[768,3072]{1,0:T(8,128)} fusion(bf16[1280,768]{1,0:T(8,128)(2,1)S(1)} %bitcast.74, bf16[1280,3072]{1,0:T(8,128)(2,1)} %fusion.13), kind=kOutput, calls=%fused_computation.49 | convolution fusion | flops 6039797760 | bytes 19267584 | tf_op jit(solution)/shard_map/cond/branch_0_fun/rm,rh->mh/dot_general | solution.py:193
  307.7 0.5 collective-permute-start.2
  308.2 0.0 slice-done
  308.2 0.0 slice-done.2
  308.2 10.1 %convolution_convert_fusion.1 = bf16[1664,768]{1,0:T(8,128)(2,1)S(1)} fusion(bf16[1664,3072]{1,0:T(8,128)(2,1)S(1)} %bitcast.60, bf16[768,3072]{1,0:T(8,128)(2,1)} %get-tuple-element.33), kind=kOutput, calls=%fused_computation.27 | convolution fusion | flops 7853015040 | bytes 17498112 | tf_op jit(solution)/shard_map/cond/branch_0_fun/rh,mh->rm/dot_general | solution.py:188
  318.3 0.0 slice-done.8
  318.3 0.0 slice-done.9
  318.3 10.8 %convolution_convert_fusion = bf16[1280,768]{1,0:T(8,128)(2,1)S(1)} fusion(bf16[1280,3072]{1,0:T(8,128)(2,1)} %fusion.13, bf16[768,3072]{1,0:T(8,128)(2,1)S(1)} %bitcast.86, bf16[768,3072]{1,0:T(8,128)(2,1)} %collective-permute-done, pred[]{:T(512)} %bitcast.4), kind=kOutput, calls=%fused_computation.26 | convolution fusion | flops 6043140096 | bytes 19267584 | tf_op jit(solution)/shard_map/cond/branch_0_fun/rh,mh->rm/dot_general | solution.py:188
  329.1 0.0 copy-start.6
  329.1 0.0 copy-start.8
  329.1 2.6 pad_maximum_fusion
  331.7 0.5 all-to-all-done.1
  332.2 4.0 all-to-all-start.3
  336.9 0.0 copy-done.6
  336.9 16.7 %gather_y.2 = (bf16[1024,768]{1,0:T(8,128)(2,1)}, bf16[1024,16]{1,0:T(8,128)(2,1)}, f32[768,16]{1,0:T(8,128)}) custom-call(bf16[2944,768]{1,0:T(8,128)(2,1)} %bitcast.6.y_ref, bf16[1024,768]{1,0:T(8,128)(2,1)S(1)} %copy-done.8, bf16[1024,768]{1,0:T(8,128)(2,1)S(1)} %copy-done.6, s32[1024,2]{1,0:T(8,128)} %copy.29.ids_ref, ...), custom_call_target="tpu_custom_call" | custom-call | flops 9261023232 | bytes 4521984 | tf_op jit(solution)/shard_map/cond/branch_0_fun/gather_y/pallas_call | solution.py:132
  353.6 40.8 %all-to-all-done.3 = bf16[16,184,768]{2,1,0:T(8,128)(2,1)} async-done(((bf16[16,184,768]{2,1,0:T(8,128)(2,1)}), bf16[16,184,768]{2,1,0:T(8,128)(2,1)}, u32[]{:S(2)}, u32[]{:S(2)}) %all-to-all-start.3) | async-done | bytes 4522016 | tf_op jit(solution)/shard_map/cond/branch_0_fun/all_to_all | solution.py:174
  394.4 10.3 %gather_dx.2 = bf16[1024,768]{1,0:T(8,128)(2,1)} custom-call(bf16[2944,768]{1,0:T(8,128)(2,1)} %bitcast.11.dx_ref, bf16[1024,16]{1,0:T(8,128)(2,1)} %get-tuple-element.40.dl_ref, bf16[768,16]{1,0:T(8,128)(2,1)} %copy.30.wg_ref, s32[1024,2]{1,0:T(8,128)} %get-tuple-element.36.slot_ref), custom_call_target="tpu_custom_call" | custom-call | flops 4630511616 | bytes 4521984 | tf_op jit(solution)/shard_map/cond/branch_0_fun/gather_dx/pallas_call | solution.py:157
  404.7 0.0 collective-permute-done.3
  404.8 18.8 %add_bitcast_fusion = f32[1,3072,768]{2,1,0:T(8,128)} fusion(f32[3072,768]{1,0:T(8,128)} %fusion.15, f32[3072,768]{1,0:T(8,128)} %collective-permute-done.3, f32[]{:T(128)S(6)} %select_n.21, bf16[1664,3072]{1,0:T(8,128)(2,1)} %get-tuple-element.155, bf16[1664,768]{1,0:T(8,128)(2,1)} %bitcast.70), kind=kOutput, calls=%fused_computation.20 | convolution fusion | flops 7858814976 | bytes 41091076 | tf_op jit(solution)/shard_map/cond/branch_0_fun/rh,rm->hm/dot_general | solution.py:192
  423.6 0.0 collective-permute-done.2
  423.6 14.8 %add_bitcast_fusion.1 = f32[1,768,3072]{2,1,0:T(8,128)} fusion(f32[768,3072]{1,0:T(8,128)} %fusion.23, f32[768,3072]{1,0:T(8,128)} %collective-permute-done.2, f32[]{:T(128)S(6)} %select_n.21, bf16[1664,768]{1,0:T(8,128)(2,1)S(1)} %bitcast.64, bf16[1664,3072]{1,0:T(8,128)(2,1)S(1)} %bitcast.62), kind=kOutput, calls=%fused_computation.21 | convolution fusion | flops 7858814976 | bytes 41091076 | tf_op jit(solution)/shard_map/cond/branch_0_fun/rm,rh->mh/dot_general | solution.py:193
  447.3 37.0 %psum.14 = f32[768,16]{1,0:T(8,128)S(1)} all-reduce(f32[768,16]{1,0:T(8,128)} %get-tuple-element.153), channel_id=1, replica_groups=mesh['ep'=16] {'ep'}, use_global_device_ids=true, to_apply=%region_5.5 | all-reduce | flops 12288 | bytes 98304 | tf_op jit(solution)/shard_map/cond/branch_0_fun/psum | solution.py:231
  484.3 0.8 copy.33
  (31 shorter events, 0.1 us)
Async XLA Ops:
  121.2 62.7 %all-to-all-start.2 = ((bf16[16,184,768]{2,1,0:T(8,128)(2,1)}), bf16[16,184,768]{2,1,0:T(8,128)(2,1)}, u32[]{:S(2)}, u32[]{:S(2)}) async-start(bf16[16,184,768]{2,1,0:T(8,128)(2,1)} %get-tuple-element.39), calls=%async_computation.2 | async-start | bytes 9043968 | tf_op jit(solution)/shard_map/cond/branch_0_fun/all_to_all | solution.py:174
  125.7 127.0 %collective-permute-start.1 = (bf16[3072,768]{1,0:T(8,128)(2,1)}, bf16[3072,768]{1,0:T(8,128)(2,1)}, u32[]{:S(2)}, u32[]{:S(2)}) collective-permute-start(bf16[3072,768]{1,0:T(8,128)(2,1)} %get-tuple-element.34), channel_id=1, source_target_pairs={{0,1},{1,0},{2,3},{3,2},{4,5},{5,4},{6,7},{7,6},{8,9},{9,8},{10,11... | collective-permute-start | bytes 14155784 | tf_op jit(solution)/shard_map/cond/branch_0_fun/ppermute | solution.py:170
  126.2 99.1 %collective-permute-start = (bf16[768,3072]{1,0:T(8,128)(2,1)}, bf16[768,3072]{1,0:T(8,128)(2,1)}, u32[]{:S(2)}, u32[]{:S(2)}) collective-permute-start(bf16[768,3072]{1,0:T(8,128)(2,1)} %get-tuple-element.33), channel_id=1, source_target_pairs={{0,1},{1,0},{2,3},{3,2},{4,5},{5,4},{6,7},{7,6},{8,9},{9,8},{10,11... | collective-permute-start | bytes 14155784 | tf_op jit(solution)/shard_map/cond/branch_0_fun/ppermute | solution.py:170
  128.7 1.4 copy-start
  183.9 26.5 %slice-start.10 = ((s8[4718592]{0:T(1024)(128)(4,1)}), s8[4194304]{0:T(1024)(128)(4,1)S(1)}, s32[]{:S(2)}) async-start(s8[4718592]{0:T(1024)(128)(4,1)} %bitcast.89), calls=%async_computation.18 | async-start | bytes 8388608 | tf_op jit(solution)/shard_map/cond
  183.9 41.4 %slice-start.6 = ((s8[4718592]{0:T(1024)(128)(4,1)}), s8[4194304]{0:T(1024)(128)(4,1)S(1)}, s32[]{:S(2)}) async-start(s8[4718592]{0:T(1024)(128)(4,1)} %bitcast.83), calls=%async_computation.14 | async-start | bytes 8388608 | tf_op jit(solution)/shard_map/cond
  185.9 24.4 %copy-start.2 = (bf16[16,104,768]{2,1,0:T(8,128)(2,1)}, bf16[16,104,768]{2,1,0:T(8,128)(2,1)S(1)}, u32[]{:S(2)}) copy-start(bf16[16,104,768]{2,1,0:T(8,128)(2,1)S(1)} %slice.12) | copy-start | bytes 7667716 | tf_op jit(solution)/shard_map/cond
  185.9 24.4 %slice-start.11 = ((s8[4718592]{0:T(1024)(128)(4,1)}), s8[524288]{0:T(1024)(128)(4,1)S(1)}, s32[]{:S(2)}) async-start(s8[4718592]{0:T(1024)(128)(4,1)} %bitcast.89), calls=%async_computation.19 | async-start | bytes 1048576 | tf_op jit(solution)/shard_map/cond
  185.9 39.4 %slice-start.7 = ((s8[4718592]{0:T(1024)(128)(4,1)}), s8[524288]{0:T(1024)(128)(4,1)S(1)}, s32[]{:S(2)}) async-start(s8[4718592]{0:T(1024)(128)(4,1)} %bitcast.83), calls=%async_computation.15 | async-start | bytes 1048576 | tf_op jit(solution)/shard_map/cond
  222.9 15.4 %copy-start.5 = (bf16[16,80,768]{2,1,0:T(8,128)(2,1)}, bf16[16,80,768]{2,1,0:T(8,128)(2,1)S(1)}, u32[]{:S(2)}) copy-start(bf16[16,80,768]{2,1,0:T(8,128)(2,1)S(1)} %slice.14) | copy-start | bytes 5898244 | tf_op jit(solution)/shard_map/cond
  225.3 13.0 %copy-start.3 = (bf16[16,80,768]{2,1,0:T(8,128)(2,1)}, bf16[16,80,768]{2,1,0:T(8,128)(2,1)S(1)}, u32[]{:S(2)}) copy-start(bf16[16,80,768]{2,1,0:T(8,128)(2,1)S(1)} %slice.15) | copy-start | bytes 5898244 | tf_op jit(solution)/shard_map/cond
  252.3 152.5 %collective-permute-start.3 = (f32[3072,768]{1,0:T(8,128)}, f32[3072,768]{1,0:T(8,128)}, u32[]{:S(2)}, u32[]{:S(2)}) collective-permute-start(f32[3072,768]{1,0:T(8,128)} %fusion.15), channel_id=1, source_target_pairs={{0,1},{1,0},{2,3},{3,2},{4,5},{5,4},{6,7},{7,6},{8,9},{9,8},{10,11... | collective-permute-start | bytes 28311560 | tf_op jit(solution)/shard_map/cond/branch_0_fun/ppermute | solution.py:170
  270.1 38.2 %slice-start = ((s8[10223616]{0:T(1024)(128)(4,1)}), s8[1835008]{0:T(1024)(128)(4,1)S(1)}, s32[]{:S(2)}) async-start(s8[10223616]{0:T(1024)(128)(4,1)} %bitcast.59), calls=%async_computation.8 | async-start | bytes 3670016 | tf_op jit(solution)/shard_map/cond
  270.1 62.1 %all-to-all-start.1 = ((bf16[16,184,768]{2,1,0:T(8,128)(2,1)}), bf16[16,184,768]{2,1,0:T(8,128)(2,1)}, u32[]{:S(2)}, u32[]{:S(2)}) async-start(bf16[16,184,768]{2,1,0:T(8,128)(2,1)} %pad_maximum_fusion.1), calls=%async_computation.1 | async-start | bytes 9043968 | tf_op jit(solution)/shard_map/cond/branch_0_fun/all_to_all | solution.py:174
  274.0 21.5 %copy-start.4 = (bf16[16,80,768]{2,1,0:T(8,128)(2,1)S(1)}, bf16[16,80,768]{2,1,0:T(8,128)(2,1)}, u32[]{:S(2)}) copy-start(bf16[16,80,768]{2,1,0:T(8,128)(2,1)} %copy-done.3) | copy-start | bytes 5898244 | tf_op jit(solution)/shard_map/cond
  274.0 34.2 %slice-start.1 = ((s8[10223616]{0:T(1024)(128)(4,1)}), s8[4194304]{0:T(1024)(128)(4,1)S(1)}, s32[]{:S(2)}) async-start(s8[10223616]{0:T(1024)(128)(4,1)} %bitcast.59), calls=%async_computation.9 | async-start | bytes 8388608 | tf_op jit(solution)/shard_map/cond
  274.0 34.2 %slice-start.2 = ((s8[10223616]{0:T(1024)(128)(4,1)}), s8[4194304]{0:T(1024)(128)(4,1)S(1)}, s32[]{:S(2)}) async-start(s8[10223616]{0:T(1024)(128)(4,1)} %bitcast.59), calls=%async_computation.10 | async-start | bytes 8388608 | tf_op jit(solution)/shard_map/cond
  295.5 22.8 %slice-start.8 = ((s8[4718592]{0:T(1024)(128)(4,1)}), s8[4194304]{0:T(1024)(128)(4,1)S(1)}, s32[]{:S(2)}) async-start(s8[4718592]{0:T(1024)(128)(4,1)} %bitcast.85), calls=%async_computation.16 | async-start | bytes 8388608 | tf_op jit(solution)/shard_map/cond
  307.7 10.6 %slice-start.9 = ((s8[4718592]{0:T(1024)(128)(4,1)}), s8[524288]{0:T(1024)(128)(4,1)S(1)}, s32[]{:S(2)}) async-start(s8[4718592]{0:T(1024)(128)(4,1)} %bitcast.85), calls=%async_computation.17 | async-start | bytes 1048576 | tf_op jit(solution)/shard_map/cond
  307.7 115.9 %collective-permute-start.2 = (f32[768,3072]{1,0:T(8,128)}, f32[768,3072]{1,0:T(8,128)}, u32[]{:S(2)}, u32[]{:S(2)}) collective-permute-start(f32[768,3072]{1,0:T(8,128)} %fusion.23), channel_id=1, source_target_pairs={{0,1},{1,0},{2,3},{3,2},{4,5},{5,4},{6,7},{7,6},{8,9},{9,8},{10,11... | collective-permute-start | bytes 28311560 | tf_op jit(solution)/shard_map/cond/branch_0_fun/ppermute | solution.py:170
  329.1 7.8 %copy-start.6 = (bf16[1024,768]{1,0:T(8,128)(2,1)S(1)}, bf16[1024,768]{1,0:T(8,128)(2,1)}, u32[]{:S(2)}) copy-start(bf16[1024,768]{1,0:T(8,128)(2,1)} %get-tuple-element.28.x_ref) | copy-start | bytes 4718596 | tf_op jit(solution)/shard_map/cond
  329.1 7.8 %copy-start.8 = (bf16[1024,768]{1,0:T(8,128)(2,1)S(1)}, bf16[1024,768]{1,0:T(8,128)(2,1)}, u32[]{:S(2)}) copy-start(bf16[1024,768]{1,0:T(8,128)(2,1)} %get-tuple-element.29.do_ref) | copy-start | bytes 4718596 | tf_op jit(solution)/shard_map/cond
  332.2 62.2 %all-to-all-start.3 = ((bf16[16,184,768]{2,1,0:T(8,128)(2,1)}), bf16[16,184,768]{2,1,0:T(8,128)(2,1)}, u32[]{:S(2)}, u32[]{:S(2)}) async-start(bf16[16,184,768]{2,1,0:T(8,128)(2,1)} %pad_maximum_fusion), calls=%async_computation.3 | async-start | bytes 9043968 | tf_op jit(solution)/shard_map/cond/branch_0_fun/all_to_all | solution.py:174
  394.4 29.2 %slice-start.3 = ((s8[10223616]{0:T(1024)(128)(4,1)}), s8[1835008]{0:T(1024)(128)(4,1)S(1)}, s32[]{:S(2)}) async-start(s8[10223616]{0:T(1024)(128)(4,1)} %bitcast.61), calls=%async_computation.11 | async-start | bytes 3670016 | tf_op jit(solution)/shard_map/cond
  404.7 18.8 %slice-start.4 = ((s8[10223616]{0:T(1024)(128)(4,1)}), s8[4194304]{0:T(1024)(128)(4,1)S(1)}, s32[]{:S(2)}) async-start(s8[10223616]{0:T(1024)(128)(4,1)} %bitcast.61), calls=%async_computation.12 | async-start | bytes 8388608 | tf_op jit(solution)/shard_map/cond
  404.7 18.9 %slice-start.5 = ((s8[10223616]{0:T(1024)(128)(4,1)}), s8[4194304]{0:T(1024)(128)(4,1)S(1)}, s32[]{:S(2)}) async-start(s8[10223616]{0:T(1024)(128)(4,1)} %bitcast.61), calls=%async_computation.13 | async-start | bytes 8388608 | tf_op jit(solution)/shard_map/cond
  404.7 18.9 %copy-start.1 = (bf16[16,104,768]{2,1,0:T(8,128)(2,1)S(1)}, bf16[16,104,768]{2,1,0:T(8,128)(2,1)}, u32[]{:S(2)}) copy-start(bf16[16,104,768]{2,1,0:T(8,128)(2,1)} %copy-done) | copy-start | bytes 7667716 | tf_op jit(solution)/shard_map/cond

commit v2 on v1

--- a/solution.py
+++ b/solution.py
@@ -7,7 +7,7 @@
 from jax.experimental.pallas import tpu as pltpu
 from jax.sharding import PartitionSpec as P
 
-BASE = 104
+BASE = 112
 EXTRA = 80
 FULL = 256
 F32 = jnp.float32
@@ -32,11 +32,24 @@
     return e0 / tot, e1 / tot
 
 
-def dispatch_kernel(base, extra, x_ref, do_ref, ids_ref, idst_ref, wg_ref, sx_ref, sdy_ref, slot_ref, gate_ref, slott_ref, gatet_ref):
+def peer_copy(src, dst, send_sem, recv_sem, peer):
+    return pltpu.make_async_remote_copy(src_ref=src, dst_ref=dst, send_sem=send_sem, recv_sem=recv_sem, device_id=(peer,), device_id_type=pl.DeviceIdType.MESH)
+
+
+def share_counts(cnt_ref, all_ref, send_sem, recv_sem, n_dev):
+    me = lax.axis_index('ep')
+    return [peer_copy(cnt_ref, all_ref.at[me], send_sem.at[i], recv_sem.at[i], lax.rem(me + i, n_dev)) for i in range(1, n_dev)]
+
+
+def dispatch_kernel(base, extra, share, x_ref, do_ref, ids_ref, idst_ref, wg_ref, sx_ref, sdy_ref, slot_ref, gate_ref, *rest):
     n_tok = x_ref.shape[0]
     n_exp = wg_ref.shape[1]
     step = pl.program_id(0)
     rows = base + extra
+    if share:
+        most_ref, slott_ref, gatet_ref, cnt_ref, all_ref, send_sem, recv_sem = rest
+    else:
+        slott_ref, gatet_ref = rest
 
     @pl.when(step == 0)
     def _():
@@ -47,6 +60,11 @@
         h0, h1 = id0 == e_col, id1 == e_col
         lower = jnp.where(c_i < r_i, 1.0, 0.0).astype(BF16)
         named = jnp.where(h0 | h1, 1.0, 0.0).astype(BF16)
+        if share:
+            cnt_ref[...] = jnp.zeros_like(cnt_ref)
+            cnt_ref[0:1, 0:n_exp] = jnp.sum(named.astype(F32), axis=0, keepdims=True)
+            for copy in share_counts(cnt_ref, all_ref, send_sem, recv_sem, n_exp):
+                copy.start()
         before = jnp.dot(lower, named, preferred_element_type=F32)
         logits = jnp.dot(x_ref[...], wg_ref[...], preferred_element_type=F32)
         pick = lambda hot, val: jnp.sum(jnp.where(hot, val, 0.0), axis=1, keepdims=True)
@@ -77,22 +95,37 @@
     sx_ref[0] = jnp.dot(sel, x_ref[...], preferred_element_type=F32).astype(BF16)
     sdy_ref[0] = (g_row * jnp.dot(sel, do_ref[...], preferred_element_type=F32)).astype(BF16)
 
-
-def dispatch(tokens, grad_out, ids, w_gate, base, extra):
+    if share:
+        @pl.when(step == n_exp - 1)
+        def _():
+            for copy in share_counts(cnt_ref, all_ref, send_sem, recv_sem, n_exp):
+                copy.wait()
+            all_ref[lax.axis_index('ep')] = cnt_ref[...]
+            most_ref[...] = jnp.max(all_ref[...], axis=0)
+
+
+def dispatch(tokens, grad_out, ids, w_gate, base, extra, share):
     n_tok, d_model = tokens.shape
     n_exp = w_gate.shape[1]
     rows = base + extra
     whole = lambda shape: pl.BlockSpec(shape, lambda i: (0,) * len(shape))
     block = pl.BlockSpec((1, rows, d_model), lambda i: (i, 0, 0))
     send = jax.ShapeDtypeStruct((n_exp, rows, d_model), BF16)
+    out_specs = [block, block, whole((n_tok, 2)), whole((n_tok, 2))]
+    out_shape = [send, send, jax.ShapeDtypeStruct((n_tok, 2), jnp.int32), jax.ShapeDtypeStruct((n_tok, 2), F32)]
+    scratch = [pltpu.VMEM((2, n_tok), jnp.int32), pltpu.VMEM((2, n_tok), F32)]
+    if share:
+        out_specs.append(whole((8, 128)))
+        out_shape.append(jax.ShapeDtypeStruct((8, 128), F32))
+        scratch += [pltpu.VMEM((8, 128), F32), pltpu.VMEM((n_exp, 8, 128), F32), pltpu.SemaphoreType.DMA((n_exp,)), pltpu.SemaphoreType.DMA((n_exp,))]
     return pl.pallas_call(
-        functools.partial(dispatch_kernel, base, extra),
+        functools.partial(dispatch_kernel, base, extra, share),
         grid=(n_exp,),
         in_specs=[whole((n_tok, d_model)), whole((n_tok, d_model)), whole((n_tok, 2)), whole((2, n_tok)), whole((d_model, n_exp))],
-        out_specs=[block, block, whole((n_tok, 2)), whole((n_tok, 2))],
-        out_shape=[send, send, jax.ShapeDtypeStruct((n_tok, 2), jnp.int32), jax.ShapeDtypeStruct((n_tok, 2), F32)],
-        scratch_shapes=[pltpu.VMEM((2, n_tok), jnp.int32), pltpu.VMEM((2, n_tok), F32)],
-        compiler_params=pltpu.CompilerParams(vmem_limit_bytes=56 * 2 ** 20),
+        out_specs=out_specs,
+        out_shape=out_shape,
+        scratch_shapes=scratch,
+        compiler_params=pltpu.CompilerParams(vmem_limit_bytes=56 * 2 ** 20, has_side_effects=share),
         cost_estimate=pl.CostEstimate(flops=4 * n_exp * rows * n_tok * d_model, bytes_accessed=4 * n_exp * rows * d_model, transcendentals=0),
         name='dispatch',
     )(tokens, grad_out, ids, ids.T, w_gate)
@@ -166,6 +199,40 @@
     )(dx_back, d_logits, w_gate, slots)
 
 
+def gate_sum_kernel(part_ref, out_ref, all_ref, send_sem, recv_sem):
+    n_dev = part_ref.shape[0]
+    me = lax.axis_index('ep')
+    peers = [(i, lax.rem(me + i, n_dev)) for i in range(1, n_dev)]
+    first = [peer_copy(part_ref.at[d], all_ref.at[me], send_sem.at[0, i], recv_sem.at[0, i], d) for i, d in peers]
+    for copy in first:
+        copy.start()
+    all_ref[me] = part_ref[me]
+    for copy in first:
+        copy.wait()
+    out_ref[me] = jnp.sum(all_ref[...], axis=0)
+    second = [peer_copy(out_ref.at[me], out_ref.at[me], send_sem.at[1, i], recv_sem.at[1, i], d) for i, d in peers]
+    for copy in second:
+        copy.start()
+    for copy in second:
+        copy.wait()
+
+
+def gate_sum(part):
+    d_model, n_exp = part.shape
+    tiles = jnp.pad(part.reshape(n_exp, -1, 128), ((0, 0), (0, 2), (0, 0)))
+    vmem = pl.BlockSpec(memory_space=pltpu.VMEM)
+    total = pl.pallas_call(
+        gate_sum_kernel,
+        in_specs=[vmem],
+        out_specs=vmem,
+        out_shape=jax.ShapeDtypeStruct(tiles.shape, F32),
+        scratch_shapes=[pltpu.VMEM(tiles.shape, F32), pltpu.SemaphoreType.DMA((2, n_exp)), pltpu.SemaphoreType.DMA((2, n_exp))],
+        compiler_params=pltpu.CompilerParams(has_side_effects=True),
+        name='gate_sum',
+    )(tiles)
+    return total[:, :6].reshape(d_model, n_exp)
+
+
 def swap(value, n_dev):
     return lax.ppermute(value, 'ep', [(d, d ^ 1) for d in range(n_dev)])
 
@@ -194,11 +261,15 @@
     return g_one, g_two
 
 
-def run_path(base, extra, tokens, grad_out, ids, w_gate, w_one, w_two, mine):
+def padded_path(tokens, grad_out, ids, w_gate, w_one, w_two, mine, *sent):
+    sent = dispatch(tokens, grad_out, ids, w_gate, FULL, 0, False)
+    return run_path(FULL, 0, tokens, grad_out, ids, w_gate, w_one, w_two, mine, *sent)
+
+
+def run_path(base, extra, tokens, grad_out, ids, w_gate, w_one, w_two, mine, send_x, send_dy, slots, gates):
     n_exp = w_gate.shape[1]
     d_model = tokens.shape[1]
     rows = base + extra
-    send_x, send_dy, slots, gates = dispatch(tokens, grad_out, ids, w_gate, base, extra)
     recv_x = exchange(send_x)
     recv_dy = exchange(send_dy)
     first = lambda v: v[:, :base].reshape(n_exp * base, d_model)
@@ -228,21 +299,19 @@
         g_one = g_one + keep * (e_one + swap(e_one, n_exp))
         g_two = g_two + keep * (e_two + swap(e_two, n_exp))
     y_out, d_logits, gw_part = gather_y(y_back, grad_out, tokens, ids, slots, gates, n_exp)
-    grad_w_gate = lax.psum(gw_part, 'ep')
+    grad_w_gate = gate_sum(gw_part)
     grad_x = gather_dx(dx_back, d_logits, w_gate, slots)
     return y_out, grad_x, g_one, g_two, grad_w_gate
 
 
 def local_block(tokens, grad_out, expert_ids, w_gate, w_in, w_out):
     n_exp = w_gate.shape[1]
-    me = lax.axis_index('ep')
-    counts = jnp.sum((expert_ids.reshape(-1)[:, None] == jnp.arange(n_exp)[None, :]).astype(jnp.int32), axis=0)
-    most = lax.pmax(counts, 'ep')
-    over = most > BASE
-    mine = over[me]
+    *sent, most = dispatch(tokens, grad_out, expert_ids, w_gate, BASE, EXTRA, True)
+    over = most[0, :n_exp] > BASE
+    mine = over[lax.axis_index('ep')]
     both = jnp.any(over.reshape(n_exp // 2, 2).all(axis=1))
-    args = (tokens, grad_out, expert_ids, w_gate, w_in[0], w_out[0], mine)
-    y_out, grad_x, g_one, g_two, g_gate = lax.cond(both, functools.partial(run_path, FULL, 0), functools.partial(run_path, BASE, EXTRA), *args)
+    args = (tokens, grad_out, expert_ids, w_gate, w_in[0], w_out[0], mine, *sent)
+    y_out, grad_x, g_one, g_two, g_gate = lax.cond(both, padded_path, functools.partial(run_path, BASE, EXTRA), *args)
     return y_out, grad_x, g_one[None], g_two[None], g_gate
 
 

time: 476 us -> 486 us (1.021); the launches traced: 485 us -> 482 us
  blocking collectives: 131 us -> 59.7 us
  Pallas kernels: 47 us -> 103 us
  local copies, waits for them, and re-layouts: 15.4 us -> 29.5 us
  waiting for transfers between devices: 76.1 us -> 67.2 us
  matrix products: 184 us -> 192 us
    pallas_call x1 -> x2, Pallas kernels: 19.9 us -> 75.2 us  [the longest x1 48.6 us: gate_sum(): pl.pallas_call(gate_sum_kernel, in_specs=[vmem], out_specs=vmem, out_shap...]
    psum x1 -> x0, blocking collectives: 37 us -> none  [run_path(): grad_w_gate = lax.psum(gw_part, 'ep')]
    pmax x1 -> x0, blocking collectives: 34.7 us -> none  [local_block(): most = lax.pmax(counts, 'ep')]
    cond x40 -> x30, local copies, waits for them, and re-layouts: 1.52 us -> 11.5 us
    all_to_all x3, waiting for transfers between devices: 76.1 us -> 67.2 us  [exchange(): return lax.all_to_all(value, 'ep', 0, 0, tiled=True)]
  transfers between devices with their start and end apart: 7 -> 7, of which waited for: 3 -> 2; matrix products, arithmetic and copies ran while one was open for 38% -> 35% of each run, Pallas kernels for 6% -> 16%
where the time goes in v2:
time: 486 us; the launch traced here: 482 us
  matrix products  192 us (40%)
  Pallas kernels  103 us (21%)
  waiting for transfers between devices  67.2 us (14%)
  blocking collectives  59.7 us (12%)
  local copies, waits for them, and re-layouts  29.5 us (6%)
  starting transfers between devices  13.3 us (3%)
  loops' own time  9.17 us (2%)
  other arithmetic  6.83 us (1%)
    all_to_all x3, waiting for transfers between devices, exchange(): return lax.all_to_all(value, 'ep', 0, 0, tiled=True)  67.2 us
    all_to_all x1, blocking collectives, exchange(): return lax.all_to_all(value, 'ep', 0, 0, tiled=True)  59.7 us
    pallas_call x1, Pallas kernels, gate_sum(): pl.pallas_call(gate_sum_kernel, in_specs=[vmem], out_specs=vmem, out_shap...  48.6 us
    dot_general x2, matrix products, expert_bwd(): d_hid = jnp.einsum('rm,hm->rh', dy_rows, w_two, preferred_element_type=F32)  46.1 us
    dot_general x2, matrix products, weight_grads(): g_two = jnp.einsum('rh,rm->hm', hid_b, dy_rows, preferred_element_type=F32)  33.9 us
    dot_general x2, matrix products, expert_fwd(): a_pre = jnp.dot(rows, w_one, preferred_element_type=F32)  32.2 us
    dot_general x2, matrix products, weight_grads(): g_one = jnp.einsum('rm,rh->mh', rows, d_pre, preferred_element_type=F32)  30.5 us
    dot_general x2, matrix products, expert_fwd(): y_rows = jnp.dot(hid_b, w_two, preferred_element_type=F32).astype(BF16)  26.9 us
  transfers between devices with their start and end apart: 7, of which 2 were waited for; matrix products, arithmetic and copies ran while one was open for 35% of the time, Pallas kernels for 16%

profile of v2, /device:TPU:0, one launch (start us, length us, event | category | flops | bytes accessed | tf_op | source)
XLA Modules:
  0.0 482.4 jit_solution(8355571322736084770)
XLA Ops:
  0.6 1.6 copy.24.wg_ref
  2.2 1.7 copy.23.ids_ref
  3.9 26.6 %dispatch.3 = (bf16[16,192,768]{2,1,0:T(8,128)(2,1)}, bf16[16,192,768]{2,1,0:T(8,128)(2,1)}, s32[1024,2]{1,0:T(8,128)}, f32[1024,2]{1,0:T(8,128)}, f32[8,128]{1,0:T(8,128)}) custom-call(bf16[1024,768]{1,0:T(8,128)(2,1)} %x_ref.1, bf16[1024,768]{1,0:T(8,128)(2,1)} %do_ref.1, s32[1024,2]{1,0:T(8,128)} %copy.23.ids_ref, s32[2,1024]{1,0:T(2,128)} %bitcast.114, ...), custom_call_target="tpu_custom_call" | custom-call | flops 9663676416 | bytes 9437184 | tf_op jit(solution)/shard_map/dispatch/pallas_call | solution.py:121
  30.6 0.7 compare_reduce_fusion
  31.3 0.7 slice.21
  31.9 0.1 gt.16
  32.0 0.1 reduce_and.9
  32.1 0.6 reduce_or.9
  33.4 447.6 %conditional.1 = (bf16[1024,768]{1,0:T(8,128)(2,1)}, bf16[1024,768]{1,0:T(8,128)(2,1)}, f32[1,3072,768]{2,1,0:T(8,128)}, f32[1,768,3072]{2,1,0:T(8,128)}, f32[768,16]{0,1:T(8,128)S(1)}) conditional(s32[]{:T(128)} %convert_element_type.42, (bf16[16,192,768]{2,1,0:T(8,128)(2,1)}, bf16[768,3072]{1,0:T(8,128)(2,1)}, bf16[3072,768]{1,0:T(8,128)(2,1)}, ...), branch_computations={%region_2.3_spmd, %region_3.4_spmd} | conditional | flops 148547567616 | bytes 675496768 | solution.py:314
  33.4 0.0 copy-start.8
  33.5 0.0 copy-start.11
  33.5 59.7 %all_to_all.32 = bf16[16,192,768]{2,1,0:T(8,128)(2,1)} all-to-all(bf16[16,192,768]{2,1,0:T(8,128)(2,1)} %get-tuple-element.51), channel_id=1, replica_groups=mesh['ep'=16] {'ep'}, dimensions={0} | all-to-all | bytes 9437184 | tf_op jit(solution)/shard_map/cond/branch_0_fun/all_to_all | solution.py:241
  93.2 3.5 all-to-all-start.2
  96.7 0.5 collective-permute-start.1
  97.2 0.1 collective-permute-start
  97.3 0.6 constant_dynamic-slice_fusion
  97.9 2.0 slice.22
  99.8 1.6 copy-done.2
  101.4 19.7 %multiply_convert_fusion = (bf16[1792,3072]{1,0:T(8,128)(2,1)}, f32[1792,3072]{1,0:T(8,128)}) fusion(bf16[1792,768]{1,0:T(8,128)(2,1)S(1)} %bitcast.101, bf16[768,3072]{1,0:T(8,128)(2,1)} %get-tuple-element.52), kind=kOutput, calls=%fused_computation.11 | convolution fusion | flops 8505262080 | bytes 40501248 | tf_op jit(solution)/shard_map/cond/branch_0_fun/dot_general | solution.py:245
  121.1 36.1 %all-to-all-done.2 = bf16[16,192,768]{2,1,0:T(8,128)(2,1)} async-done(((bf16[16,192,768]{2,1,0:T(8,128)(2,1)}), bf16[16,192,768]{2,1,0:T(8,128)(2,1)}, u32[]{:S(2)}, u32[]{:S(2)}) %all-to-all-start.2) | async-done | bytes 4718624 | tf_op jit(solution)/shard_map/cond/branch_0_fun/all_to_all | solution.py:241
  157.1 2.1 slice.24
  159.3 0.0 slice-start.1
  159.3 25.4 %fusion.6 = bf16[1792,3072]{1,0:T(8,128)(2,1)} fusion(f32[1792,3072]{1,0:T(8,128)} %get-tuple-element.163, bf16[1792,768]{1,0:T(8,128)(2,1)S(1)} %bitcast.99, bf16[3072,768]{1,0:T(8,128)(2,1)} %get-tuple-element.53), kind=kOutput, calls=%fused_computation.10 | convolution fusion | flops 8565817344 | bytes 40501248 | tf_op jit(solution)/shard_map/cond/branch_0_fun/rm,hm->rh/dot_general | solution.py:253
  184.7 0.0 slice-done
  184.7 11.6 %convolution_convert_fusion.1 = bf16[1792,768]{1,0:T(8,128)(2,1)S(1)} fusion(bf16[1792,3072]{1,0:T(8,128)(2,1)} %fusion.6, bf16[768,3072]{1,0:T(8,128)(2,1)S(1)} %bitcast.118), kind=kOutput, calls=%fused_computation.35 | convolution fusion | flops 8457093120 | bytes 18481152 | tf_op jit(solution)/shard_map/cond/branch_0_fun/rh,mh->rm/dot_general | solution.py:255
  196.3 1.7 slice.23
  198.0 0.0 copy-start.6
  198.0 2.4 slice.25
  200.4 13.5 %convolution_convert_fusion.3 = bf16[1792,768]{1,0:T(8,128)(2,1)S(1)} fusion(bf16[1792,3072]{1,0:T(8,128)(2,1)} %get-tuple-element.162, bf16[3072,768]{1,0:T(8,128)(2,1)} %get-tuple-element.53), kind=kOutput, calls=%fused_computation.37 | convolution fusion | flops 8457093120 | bytes 18481152 | tf_op jit(solution)/shard_map/cond/branch_0_fun/dot_general | solution.py:248
  214.0 0.0 collective-permute-done
  214.0 0.0 copy-done.6
  214.0 12.5 %fusion.19 = f32[3072,1280]{1,0:T(8,128)} fusion(bf16[1280,768]{1,0:T(8,128)(2,1)S(1)} %bitcast.108, bf16[768,3072]{1,0:T(8,128)(2,1)S(1)} %bitcast.118, bf16[768,3072]{1,0:T(8,128)(2,1)} %collective-permute-done, pred[]{:T(512)} %bitcast.2), kind=kOutput, calls=%fused_computation.38 | convolution fusion | flops 6042157056 | bytes 27131904 | tf_op jit(solution)/shard_map/cond/branch_0_fun/dot_general | solution.py:245
  226.5 0.0 collective-permute-done.1
  226.5 20.7 %fusion.13 = bf16[1280,3072]{0,1:T(8,128)(2,1)} fusion(f32[3072,1280]{1,0:T(8,128)} %fusion.19, bf16[1280,768]{1,0:T(8,128)(2,1)S(1)} %bitcast.106, bf16[3072,768]{1,0:T(8,128)(2,1)} %get-tuple-element.53, bf16[3072,768]{1,0:T(8,128)(2,1)} %collective-permute-done.1, pred[]{:T(512)} %bitcast.2), kind=kOutput, calls=%fused_computation.18 | convolution fusion | flops 6120800256 | bytes 34996224 | tf_op jit(solution)/shard_map/cond/branch_0_fun/rm,hm->rh/dot_general | solution.py:253
  247.2 11.9 %convolution_bitcast_fusion = f32[768,3072]{0,1:T(8,128)} fusion(bf16[1280,3072]{0,1:T(8,128)(2,1)} %fusion.13, bf16[1280,768]{1,0:T(8,128)(2,1)} %bitcast.109), kind=kOutput, calls=%fused_computation.29 | convolution fusion | flops 6039797760 | bytes 19267584 | tf_op jit(solution)/shard_map/cond/branch_0_fun/rm,rh->mh/dot_general | solution.py:260
  259.0 0.5 collective-permute-start.2
  259.6 13.4 %convolution_convert_fusion.2 = bf16[1280,768]{1,0:T(8,128)(2,1)S(1)} fusion(bf16[3072,768]{1,0:T(8,128)(2,1)} %get-tuple-element.53, bf16[3072,768]{1,0:T(8,128)(2,1)} %collective-permute-done.1, pred[]{:T(512)} %bitcast.2, f32[3072,1280]{1,0:T(8,128)} %fusion.19), kind=kOutput, calls=%fused_computation.36 | convolution fusion | flops 6078529536 | bytes 27131904 | tf_op jit(solution)/shard_map/cond/branch_0_fun/dot_general | solution.py:248
  273.0 2.6 pad_maximum_fusion
  275.6 4.1 all-to-all-start.1
  279.8 15.4 %fusion.20 = f32[3072,768]{1,0:T(8,128)} fusion(bf16[1280,768]{1,0:T(8,128)(2,1)} %bitcast.107, f32[3072,1280]{1,0:T(8,128)} %fusion.19), kind=kOutput, calls=%fused_computation.41 | convolution fusion | flops 6075187200 | bytes 27131904 | tf_op jit(solution)/shard_map/cond/branch_0_fun/rh,rm->hm/dot_general | solution.py:259
  295.2 0.5 collective-permute-start.3
  295.7 10.8 %convolution_convert_fusion = bf16[1280,768]{1,0:T(8,128)(2,1)S(1)} fusion(bf16[1280,3072]{0,1:T(8,128)(2,1)} %fusion.13, bf16[768,3072]{1,0:T(8,128)(2,1)} %get-tuple-element.52, bf16[768,3072]{1,0:T(8,128)(2,1)} %collective-permute-done, pred[]{:T(512)} %bitcast.2), kind=kOutput, calls=%fused_computation.34 | convolution fusion | flops 6043140096 | bytes 19267584 | tf_op jit(solution)/shard_map/cond/branch_0_fun/rh,mh->rm/dot_general | solution.py:255
  306.5 0.0 copy-start.9
  306.5 0.0 copy-start.12
  306.5 2.7 pad_maximum_fusion.1
  309.2 31.2 %all-to-all-done.1 = bf16[16,192,768]{2,1,0:T(8,128)(2,1)} async-done(((bf16[16,192,768]{2,1,0:T(8,128)(2,1)}), bf16[16,192,768]{2,1,0:T(8,128)(2,1)}, u32[]{:S(2)}, u32[]{:S(2)}) %all-to-all-start.1) | async-done | bytes 4718624 | tf_op jit(solution)/shard_map/cond/branch_0_fun/all_to_all | solution.py:241
  340.4 4.1 all-to-all-start.3
  344.5 0.8 copy.26.wg_ref
  345.3 1.0 copy.25.ids_ref
  347.0 16.8 %gather_y.2 = (bf16[1024,768]{1,0:T(8,128)(2,1)}, bf16[1024,16]{1,0:T(8,128)(2,1)}, f32[768,16]{1,0:T(8,128)}) custom-call(bf16[3072,768]{1,0:T(8,128)(2,1)} %bitcast.6.y_ref, bf16[1024,768]{1,0:T(8,128)(2,1)S(1)} %copy-done.16, bf16[1024,768]{1,0:T(8,128)(2,1)S(1)} %copy-done.14, s32[1024,2]{1,0:T(8,128)} %copy.25.ids_ref, ...), custom_call_target="tpu_custom_call" | custom-call | flops 9663676416 | bytes 4718592 | tf_op jit(solution)/shard_map/cond/branch_0_fun/gather_y/pallas_call | solution.py:165
  363.8 1.2 reshape.68
  364.9 0.6 pad.5.part_ref
  365.6 48.6 %gate_sum.2 = f32[16,8,128]{2,1,0:T(8,128)} custom-call(f32[16,8,128]{2,1,0:T(8,128)} %pad.5.part_ref), custom_call_target="tpu_custom_call" | custom-call | tf_op jit(solution)/shard_map/cond/branch_0_fun/gate_sum/pallas_call | solution.py:224
  414.2 1.0 reshape.69
  415.2 0.1 copy.33
  415.3 0.0 all-to-all-done.3
  415.3 10.5 %gather_dx.2 = bf16[1024,768]{1,0:T(8,128)(2,1)} custom-call(bf16[3072,768]{1,0:T(8,128)(2,1)} %bitcast.12.dx_ref, bf16[1024,16]{1,0:T(8,128)(2,1)} %get-tuple-element.63.dl_ref, bf16[768,16]{1,0:T(8,128)(2,1)} %copy.26.wg_ref, s32[1024,2]{1,0:T(8,128)} %get-tuple-element.59.slot_ref), custom_call_target="tpu_custom_call" | custom-call | flops 4831838208 | bytes 4718592 | tf_op jit(solution)/shard_map/cond/branch_0_fun/gather_dx/pallas_call | solution.py:190
  425.8 0.0 collective-permute-done.2
  425.8 18.6 %fusion.18 = f32[1,768,3072]{1,2,0:T(8,128)} fusion(f32[768,3072]{0,1:T(8,128)} %convolution_bitcast_fusion, f32[768,3072]{0,1:T(8,128)} %collective-permute-done.2, bf16[1792,3072]{1,0:T(8,128)(2,1)} %fusion.6, bf16[1792,768]{1,0:T(8,128)(2,1)S(1)} %bitcast.102, f32[]{:T(128)S(6)} %select_n.23), kind=kOutput, calls=%fused_computation.27 | convolution fusion | flops 8462794752 | bytes 42074116 | tf_op jit(solution)/shard_map/cond/branch_0_fun/rm,rh->mh/dot_general | solution.py:260
  444.5 9.7 %copy.31 = f32[1,768,3072]{2,1,0:T(8,128)} copy(f32[1,768,3072]{1,2,0:T(8,128)} %fusion.18) | data formatting | bytes 18874368 | tf_op jit(solution)/shard_map/cond
  454.2 0.0 collective-permute-done.3
  454.2 18.5 %add_bitcast_fusion = f32[1,3072,768]{2,1,0:T(8,128)} fusion(f32[3072,768]{1,0:T(8,128)} %fusion.20, f32[3072,768]{1,0:T(8,128)} %collective-permute-done.3, f32[]{:T(128)S(6)} %select_n.23, bf16[1792,3072]{1,0:T(8,128)(2,1)} %get-tuple-element.162, bf16[1792,768]{1,0:T(8,128)(2,1)S(1)} %bitcast.100), kind=kOutput, calls=%fused_computation.28 | convolution fusion | flops 8462794752 | bytes 42074116 | tf_op jit(solution)/shard_map/cond/branch_0_fun/rh,rm->hm/dot_general | solution.py:259
  481.0 0.0 copy-start.13
  481.0 0.6 copy-done.13
  (25 shorter events, 0.1 us)
Async XLA Ops:
  3.9 28.9 %copy-start.7 = (bf16[768,16]{0,1:T(8,128)(2,1)S(1)}, bf16[768,16]{0,1:T(8,128)(2,1)}, u32[]{:S(2)}) copy-start(bf16[768,16]{0,1:T(8,128)(2,1)} %param.11) | copy-start | bytes 73732
  3.9 28.9 %copy-start.10 = (s32[1024,2]{0,1:T(2,128)S(1)}, s32[1024,2]{0,1:T(2,128)}, u32[]{:S(2)}) copy-start(s32[1024,2]{0,1:T(2,128)} %param.10) | copy-start | bytes 24580
  33.4 59.8 %copy-start.8 = (bf16[768,16]{0,1:T(8,128)(2,1)}, bf16[768,16]{0,1:T(8,128)(2,1)S(1)}, u32[]{:S(2)}) copy-start(bf16[768,16]{0,1:T(8,128)(2,1)S(1)} %get-tuple-element.148) | copy-start | bytes 73732 | tf_op jit(solution)/shard_map/cond
  33.5 59.7 %copy-start.11 = (s32[1024,2]{0,1:T(2,128)}, s32[1024,2]{0,1:T(2,128)S(1)}, u32[]{:S(2)}) copy-start(s32[1024,2]{0,1:T(2,128)S(1)} %get-tuple-element.144) | copy-start | bytes 24580 | tf_op jit(solution)/shard_map/cond
  93.2 63.9 %all-to-all-start.2 = ((bf16[16,192,768]{2,1,0:T(8,128)(2,1)}), bf16[16,192,768]{2,1,0:T(8,128)(2,1)}, u32[]{:S(2)}, u32[]{:S(2)}) async-start(bf16[16,192,768]{2,1,0:T(8,128)(2,1)} %get-tuple-element.62), calls=%async_computation.2 | async-start | bytes 9437184 | tf_op jit(solution)/shard_map/cond/branch_0_fun/all_to_all | solution.py:241
  96.7 129.8 %collective-permute-start.1 = (bf16[3072,768]{1,0:T(8,128)(2,1)}, bf16[3072,768]{1,0:T(8,128)(2,1)}, u32[]{:S(2)}, u32[]{:S(2)}) collective-permute-start(bf16[3072,768]{1,0:T(8,128)(2,1)} %get-tuple-element.53), channel_id=1, source_target_pairs={{0,1},{1,0},{2,3},{3,2},{4,5},{5,4},{6,7},{7,6},{8,9},{9,8},{10,11... | collective-permute-start | bytes 14155784 | tf_op jit(solution)/shard_map/cond/branch_0_fun/ppermute | solution.py:237
  97.2 116.8 %collective-permute-start = (bf16[768,3072]{1,0:T(8,128)(2,1)}, bf16[768,3072]{1,0:T(8,128)(2,1)}, u32[]{:S(2)}, u32[]{:S(2)}) collective-permute-start(bf16[768,3072]{1,0:T(8,128)(2,1)} %get-tuple-element.52), channel_id=1, source_target_pairs={{0,1},{1,0},{2,3},{3,2},{4,5},{5,4},{6,7},{7,6},{8,9},{9,8},{10,11... | collective-permute-start | bytes 14155784 | tf_op jit(solution)/shard_map/cond/branch_0_fun/ppermute | solution.py:237
  99.8 1.6 copy-start.2
  157.1 27.5 %slice-start = ((s8[4718592]{0:T(1024)(128)(4,1)}), s8[4194304]{0:T(1024)(128)(4,1)S(1)}, s32[]{:S(2)}) async-start(s8[4718592]{0:T(1024)(128)(4,1)} %bitcast.117), calls=%async_computation.8 | async-start | bytes 8388608 | tf_op jit(solution)/shard_map/cond
  159.3 25.4 %copy-start = (bf16[16,112,768]{2,1,0:T(8,128)(2,1)}, bf16[16,112,768]{2,1,0:T(8,128)(2,1)S(1)}, u32[]{:S(2)}) copy-start(bf16[16,112,768]{2,1,0:T(8,128)(2,1)S(1)} %slice.24) | copy-start | bytes 8257540 | tf_op jit(solution)/shard_map/cond
  159.3 25.4 %slice-start.1 = ((s8[4718592]{0:T(1024)(128)(4,1)}), s8[524288]{0:T(1024)(128)(4,1)S(1)}, s32[]{:S(2)}) async-start(s8[4718592]{0:T(1024)(128)(4,1)} %bitcast.117), calls=%async_computation.9 | async-start | bytes 1048576 | tf_op jit(solution)/shard_map/cond
  198.0 16.0 %copy-start.6 = (bf16[16,80,768]{2,1,0:T(8,128)(2,1)}, bf16[16,80,768]{2,1,0:T(8,128)(2,1)S(1)}, u32[]{:S(2)}) copy-start(bf16[16,80,768]{2,1,0:T(8,128)(2,1)S(1)} %slice.23) | copy-start | bytes 5898244 | tf_op jit(solution)/shard_map/cond
  200.4 26.1 %copy-start.5 = (bf16[16,80,768]{2,1,0:T(8,128)(2,1)}, bf16[16,80,768]{2,1,0:T(8,128)(2,1)S(1)}, u32[]{:S(2)}) copy-start(bf16[16,80,768]{2,1,0:T(8,128)(2,1)S(1)} %slice.25) | copy-start | bytes 5898244 | tf_op jit(solution)/shard_map/cond
  259.0 166.8 %collective-permute-start.2 = (f32[768,3072]{0,1:T(8,128)}, f32[768,3072]{0,1:T(8,128)}, u32[]{:S(2)}, u32[]{:S(2)}) collective-permute-start(f32[768,3072]{0,1:T(8,128)} %convolution_bitcast_fusion), channel_id=1, source_target_pairs={{0,1},{1,0},{2,3},{3,2},{4,5},{5,4},{6,7},{7,6},{8,9},{9,8},{10,11... | collective-permute-start | bytes 28311560 | tf_op jit(solution)/shard_map/cond/branch_0_fun/ppermute | solution.py:237
  275.6 64.7 %all-to-all-start.1 = ((bf16[16,192,768]{2,1,0:T(8,128)(2,1)}), bf16[16,192,768]{2,1,0:T(8,128)(2,1)}, u32[]{:S(2)}, u32[]{:S(2)}) async-start(bf16[16,192,768]{2,1,0:T(8,128)(2,1)} %pad_maximum_fusion), calls=%async_computation.1 | async-start | bytes 9437184 | tf_op jit(solution)/shard_map/cond/branch_0_fun/all_to_all | solution.py:241
  295.2 159.0 %collective-permute-start.3 = (f32[3072,768]{1,0:T(8,128)}, f32[3072,768]{1,0:T(8,128)}, u32[]{:S(2)}, u32[]{:S(2)}) collective-permute-start(f32[3072,768]{1,0:T(8,128)} %fusion.20), channel_id=1, source_target_pairs={{0,1},{1,0},{2,3},{3,2},{4,5},{5,4},{6,7},{7,6},{8,9},{9,8},{10,11... | collective-permute-start | bytes 28311560 | tf_op jit(solution)/shard_map/cond/branch_0_fun/ppermute | solution.py:237
  306.5 38.0 %copy-start.9 = (bf16[768,16]{0,1:T(8,128)(2,1)S(1)}, bf16[768,16]{0,1:T(8,128)(2,1)}, u32[]{:S(2)}) copy-start(bf16[768,16]{0,1:T(8,128)(2,1)} %copy-done.8) | copy-start | bytes 73732 | tf_op jit(solution)/shard_map/cond
  306.5 38.8 %copy-start.12 = (s32[1024,2]{0,1:T(2,128)S(1)}, s32[1024,2]{0,1:T(2,128)}, u32[]{:S(2)}) copy-start(s32[1024,2]{0,1:T(2,128)} %copy-done.11) | copy-start | bytes 24580 | tf_op jit(solution)/shard_map/cond
  309.2 37.8 %copy-start.14 = (bf16[1024,768]{1,0:T(8,128)(2,1)S(1)}, bf16[1024,768]{1,0:T(8,128)(2,1)}, u32[]{:S(2)}) copy-start(bf16[1024,768]{1,0:T(8,128)(2,1)} %get-tuple-element.57.x_ref) | copy-start | bytes 4718596 | tf_op jit(solution)/shard_map/cond
  309.2 37.8 %copy-start.16 = (bf16[1024,768]{1,0:T(8,128)(2,1)S(1)}, bf16[1024,768]{1,0:T(8,128)(2,1)}, u32[]{:S(2)}) copy-start(bf16[1024,768]{1,0:T(8,128)(2,1)} %get-tuple-element.56.do_ref) | copy-start | bytes 4718596 | tf_op jit(solution)/shard_map/cond
  340.4 74.9 %all-to-all-start.3 = ((bf16[16,192,768]{2,1,0:T(8,128)(2,1)}), bf16[16,192,768]{2,1,0:T(8,128)(2,1)}, u32[]{:S(2)}, u32[]{:S(2)}) async-start(bf16[16,192,768]{2,1,0:T(8,128)(2,1)} %pad_maximum_fusion.1), calls=%async_computation.3 | async-start | bytes 9437184 | tf_op jit(solution)/shard_map/cond/branch_0_fun/all_to_all | solution.py:241
  365.6 60.2 %copy-start.3 = (bf16[16,112,768]{2,1,0:T(8,128)(2,1)S(1)}, bf16[16,112,768]{2,1,0:T(8,128)(2,1)}, u32[]{:S(2)}) copy-start(bf16[16,112,768]{2,1,0:T(8,128)(2,1)} %copy-done.2) | copy-start | bytes 8257540 | tf_op jit(solution)/shard_map/cond
  444.5 9.7 %copy-start.1 = (bf16[16,112,768]{2,1,0:T(8,128)(2,1)S(1)}, bf16[16,112,768]{2,1,0:T(8,128)(2,1)}, u32[]{:S(2)}) copy-start(bf16[16,112,768]{2,1,0:T(8,128)(2,1)} %copy-done) | copy-start | bytes 8257540 | tf_op jit(solution)/shard_map/cond
  481.0 0.6 copy-start.13
